TPU v7x, 8 devices: a whole 2x2x1 slice. The times are simulated.
8 devices in a mesh: dp: 1 (over z), x: 8 (over y, x, core).
Axes of the slice: x: 2, y: 2, z: 1, core: 2. Of those that a mesh axis runs over, the one named last changes fastest.
Arguments:
- c_raw: bfloat16 [96, 6144, 512], P('dp', 'x')
- k_raw: bfloat16 [96, 6144, 64], P('dp', 'x')
- norm_gain: bfloat16 [512], replicated
- rope_cos: float32 [6144, 32], P('x')
- rope_sin: float32 [6144, 32], P('x')
- seq_lens: int32 [96], P('dp')
- q_lat: bfloat16 [96, 128, 512], P(('dp', 'x'))
- q_rope: bfloat16 [96, 128, 64], P(('dp', 'x'))
Outputs:
- output 1: bfloat16 [96, 6144, 512], P(('dp', 'x'))
- output 2: bfloat16 [96, 6144, 64], P(('dp', 'x'))
- output 3: bfloat16 [96, 128, 512], P(('dp', 'x'))
All inputs are finite; a program needn't handle non-finite values.
Results may differ from a plain program's by a relative error of at most 0.00562413.
Values are sent between devices in bfloat16 or wider.
A program may use at most 1 GiB of HBM per device.

v0:
```python
import jax
import jax.numpy as jnp
import numpy as np
from jax import lax
from jax.experimental import pallas as pl
from jax.experimental.pallas import tpu as pltpu
from jax.sharding import PartitionSpec as P

NORM_EPS = 1e-6
N = 8
CHIPS = 4
REQ = 12
SEQ = 768
RANK = 512
ROPE = 64
HEADS = 128
UNIT = 256
PER = SEQ // UNIT
PIECES = RANK // 128
HALVES = UNIT // 128
ROWS = PIECES * UNIT + HALVES * ROPE
SLOTS = 2 * REQ * PER
NONE = 10**6
ATTN_SCALE = (RANK + ROPE) ** -0.5
DEPTH = 2


SPILL = 8
SPILLERS = (2, 3)


class Plan:
    def __init__(self, chunks):
        self.chunks = chunks
        self.starts = np.cumsum([0] + [c[0] for c in chunks])[:-1]
        assert sum(c[0] for c in chunks) == SLOTS
        self.slot = np.full((N, CHIPS, SLOTS), NONE, np.int32)
        self.cap = np.zeros((N, CHIPS), np.int32)
        for s in range(N):
            for q in range(CHIPS):
                spills = s in SPILLERS and q in (2, 3)
                for c in sorted(range(len(chunks)), key=lambda c: spills and c == SPILL):
                    chunk, start, width = chunks[c], self.starts[c], chunks[c][0]
                    if q == 0 or s in chunk[q + 1]:
                        self.slot[s, q, start : start + width] = self.cap[s, q] + np.arange(width)
                        self.cap[s, q] += width


ALL = (0, 1, 2, 3, 4, 5, 6, 7)
UP = (0, 1, 2, 3)
LOW = (4, 5, 6, 7)


NO_CHIP1 = (0, 1, 4, 5, 6, 7)
NO_3 = (0, 1, 2, 4, 5, 6, 7)


def direct(width):
    return width, "direct", ALL, ALL, ALL


def relay(width):
    return width, "relay", UP, ALL, UP


def no_chip1(width):
    return width, "direct", ALL, NO_CHIP1, NO_CHIP1


def no_3(width):
    return width, "direct", ALL, NO_3, NO_3


def end(width):
    return width, "direct", UP, ALL, UP


PLAN = Plan(
    [direct(2), direct(4), direct(6), relay(7), no_chip1(5), relay(6), no_chip1(4), no_3(9)]
    + [direct(8), direct(8), direct(7), end(4), end(2)]
)
ROOM = PLAN.chunks[SPILL][0]
EXTRA = 4


def norm_pack(width, start, stride, tabs, c_raw, k_t, gain, cos_t, sin_t, after):
    steps = CHIPS * width

    def kernel(req_ref, unit_ref, ok_ref, c_ref, k_ref, g_ref, cos_ref, sin_ref, *refs):
        outs, (buf, sem) = refs[len(after) : len(after) + CHIPS], refs[-2:]
        n = pl.program_id(0)
        q, j = n // width, n % width
        ok_at = lambda m: ok_ref[m // width * stride + start + m % width] > 0
        drain = lambda m: pltpu.make_async_copy(buf.at[m % 2], outs[0].at[0], sem.at[m % 2]).wait()
        slot = n % 2

        @pl.when((n >= 2) & ok_at(jnp.maximum(n - 2, 0)))
        def _():
            drain(n)

        @pl.when(ok_at(n))
        def _():
            key = k_ref[0].astype(jnp.float32)
            lo, hi = key[: ROPE // 2], key[ROPE // 2 :]
            cos, sin = cos_ref[...], sin_ref[...]
            rot = jnp.concatenate([lo * cos - hi * sin, hi * cos + lo * sin], axis=0).astype(jnp.bfloat16)
            for p in range(HALVES):
                at = PIECES * UNIT + p * ROPE
                buf[slot, at : at + ROPE, :] = rot[:, p * 128 : (p + 1) * 128]
                x = c_ref[0, p * 128 : (p + 1) * 128, :].astype(jnp.float32)
                inv = lax.rsqrt(jnp.mean(x * x, axis=-1, keepdims=True) + NORM_EPS)
                y = (x * inv * g_ref[...].astype(jnp.float32)).astype(jnp.bfloat16)
                for i in range(PIECES):
                    at = i * UNIT + p * 128
                    buf[slot, at : at + 128, :] = y[:, i * 128 : (i + 1) * 128]
            for mine in range(CHIPS):

                @pl.when(q == mine)
                def _(mine=mine):
                    pltpu.make_async_copy(buf.at[slot], outs[mine].at[j], sem.at[slot]).start()

        @pl.when(n == steps - 1)
        def _():
            @pl.when(ok_at(n - 1))
            def _():
                drain(n - 1)

            @pl.when(ok_at(n))
            def _():
                drain(n)

    def at(n):
        return n // width * stride + start + n % width

    grid_spec = pltpu.PrefetchScalarGridSpec(
        num_scalar_prefetch=3,
        grid=(steps,),
        in_specs=[
            pl.BlockSpec((1, UNIT, RANK), lambda n, req, unit, ok: (req[at(n)], unit[at(n)], 0)),
            pl.BlockSpec((1, ROPE, UNIT), lambda n, req, unit, ok: (req[at(n)], 0, unit[at(n)])),
            pl.BlockSpec((1, RANK), lambda n, *_: (0, 0)),
            pl.BlockSpec((ROPE // 2, UNIT), lambda n, req, unit, ok: (0, unit[at(n)])),
            pl.BlockSpec((ROPE // 2, UNIT), lambda n, req, unit, ok: (0, unit[at(n)])),
        ]
        + [pl.BlockSpec(memory_space=pl.ANY)] * len(after),
        out_specs=[pl.BlockSpec(memory_space=pl.ANY)] * CHIPS,
        scratch_shapes=[pltpu.VMEM((2, ROWS, 128), jnp.bfloat16), pltpu.SemaphoreType.DMA((2,))],
    )
    return pl.pallas_call(
        kernel,
        grid_spec=grid_spec,
        out_shape=[jax.ShapeDtypeStruct((width, ROWS, 128), jnp.bfloat16)] * CHIPS,
        cost_estimate=pl.CostEstimate(flops=width * 10**8, bytes_accessed=width * 4 * 589824, transcendentals=0),
        name="norm_pack",
    )(*tabs, c_raw, k_t, gain, cos_t, sin_t, *after)


def attend(chunk, start, first, last, counts, codes, parts, q_lat, q_rope_t, caches, state):
    total = len(parts)

    def kernel(count_ref, code_ref, *refs):
        part_refs, (qa_ref, qr_ref) = refs[:total], refs[total : total + 2]
        old_ref = None if first else refs[total + 4]
        outs = refs[total + (4 if first else 5) :]
        c_out, k_out, st_ref = outs[:3]
        buf, c_buf, k_buf, in_sem, c_sem, k_sem = outs[-6:]
        steps = count_ref[chunk]

        def fetch(n):
            code = code_ref[start + n]
            part, place = code // 2**22, code // 2**18 % 16
            for k in range(total):

                @pl.when(part == k)
                def _(k=k):
                    pltpu.make_async_copy(part_refs[k].at[place], buf.at[n % 3], in_sem.at[n % 3]).start()

        def drain(slot):
            pltpu.make_async_copy(c_buf.at[slot], c_out.at[0, pl.ds(0, UNIT), :], c_sem.at[slot]).wait()
            pltpu.make_async_copy(k_buf.at[slot], k_out.at[0, :, pl.ds(0, UNIT)], k_sem.at[slot]).wait()

        def step(n, _):
            code = code_ref[start + n]
            left, r = code // 2**9 % 2**9, code // 2**5 % 16
            at = pl.ds(pl.multiple_of(code % 2**5 * UNIT, UNIT), UNIT)
            slot = n % 2

            @pl.when(n + 2 < steps)
            def _():
                fetch(n + 2)

            pltpu.make_async_copy(part_refs[0].at[0], buf.at[n % 3], in_sem.at[n % 3]).wait()

            @pl.when(n >= 2)
            def _():
                drain(slot)

            row_ok = lax.broadcasted_iota(jnp.int32, (UNIT, 1), 0) < left
            lane_ok = lax.broadcasted_iota(jnp.int32, (1, UNIT), 1) < left
            for i in range(PIECES):
                piece = jnp.where(row_ok, buf[n % 3, i * UNIT : (i + 1) * UNIT, :].astype(jnp.float32), 0.0)
                c_buf[slot, :, i * 128 : (i + 1) * 128] = piece.astype(jnp.bfloat16)
            for p in range(HALVES):
                base = PIECES * UNIT + p * ROPE
                key = buf[n % 3, base : base + ROPE, :].astype(jnp.float32)
                key = jnp.where(lane_ok[:, p * 128 : (p + 1) * 128], key, 0.0)
                k_buf[slot, :, p * 128 : (p + 1) * 128] = key.astype(jnp.bfloat16)
            pltpu.make_async_copy(c_buf.at[slot], c_out.at[r, at, :], c_sem.at[slot]).start()
            pltpu.make_async_copy(k_buf.at[slot], k_out.at[r, :, at], k_sem.at[slot]).start()

            c = c_buf[slot]
            scores = lax.dot_general(qa_ref[r], c, (((1,), (1,)), ((), ())), preferred_element_type=jnp.float32)
            scores += lax.dot_general(qr_ref[r], k_buf[slot], (((0,), (0,)), ((), ())), preferred_element_type=jnp.float32)
            scores = jnp.where(lane_ok, scores * ATTN_SCALE, -1e30)
            l_old = st_ref[r, :, RANK : RANK + 1]
            m_old = st_ref[r, :, RANK + 128 : RANK + 129]
            m_new = jnp.maximum(m_old, jnp.max(scores, axis=-1, keepdims=True))
            weights = jnp.exp(scores - m_new)
            decay = jnp.exp(m_old - m_new)
            l_new = l_old * decay + jnp.sum(weights, axis=-1, keepdims=True)
            st_ref[r, :, RANK : RANK + 128] = jnp.broadcast_to(l_new, (HEADS, 128))
            st_ref[r, :, RANK + 128 :] = jnp.broadcast_to(m_new, (HEADS, 128))
            st_ref[r, :, :RANK] = st_ref[r, :, :RANK] * decay + jnp.dot(
                weights.astype(jnp.bfloat16), c, preferred_element_type=jnp.float32
            )
            return 0

        @pl.when(steps > 0)
        def _():
            fetch(0)

        @pl.when(steps > 1)
        def _():
            fetch(1)

        if first:
            st_ref[:, :, : RANK + 128] = jnp.zeros((REQ, HEADS, RANK + 128), jnp.float32)
            st_ref[:, :, RANK + 128 :] = jnp.full((REQ, HEADS, 128), -1e30, jnp.float32)
        else:
            st_ref[...] = old_ref[...]
        lax.fori_loop(0, steps, step, 0)

        @pl.when(steps > 1)
        def _():
            drain(steps % 2)

        @pl.when(steps > 0)
        def _():
            drain((steps + 1) % 2)

        if last:
            o_ref = outs[3]

            def finish(r, _):
                o_ref[r] = (st_ref[r, :, :RANK] / st_ref[r, :, RANK : RANK + 1]).astype(jnp.bfloat16)
                return 0

            lax.fori_loop(0, REQ, finish, 0)

    smem, vmem, anywhere = (pl.BlockSpec(memory_space=m) for m in (pltpu.SMEM, pltpu.VMEM, pl.ANY))
    state_shape = (REQ, HEADS, RANK + 256)
    in_specs = [smem] * 2 + [anywhere] * total + [vmem] * 2 + [anywhere] * 2
    operands = [counts, codes, *parts, q_lat, q_rope_t]
    aliases = {len(operands): 0, len(operands) + 1: 1}
    operands += list(caches)
    if not first:
        in_specs.append(vmem)
        operands.append(state)
    out_specs = [anywhere, anywhere, vmem]
    out_shape = [jax.ShapeDtypeStruct(c.shape, c.dtype) for c in caches] + [jax.ShapeDtypeStruct(state_shape, jnp.float32)]
    if last:
        out_specs.append(vmem)
        out_shape.append(jax.ShapeDtypeStruct((REQ, HEADS, RANK), jnp.bfloat16))
    return pl.pallas_call(
        kernel,
        in_specs=in_specs,
        out_specs=out_specs,
        out_shape=out_shape,
        scratch_shapes=[
            pltpu.VMEM((3, ROWS, 128), jnp.bfloat16),
            pltpu.VMEM((2, UNIT, RANK), jnp.bfloat16),
            pltpu.VMEM((2, ROPE, UNIT), jnp.bfloat16),
            pltpu.SemaphoreType.DMA((3,)),
            pltpu.SemaphoreType.DMA((2,)),
            pltpu.SemaphoreType.DMA((2,)),
        ],
        input_output_aliases=aliases,
        cost_estimate=pl.CostEstimate(flops=2 * 10**8, bytes_accessed=8 * 589824, transcendentals=0),
        name="attend",
    )(*operands)


def blank_caches(lens):
    def kernel(len_ref, c_ref, k_ref, c_zero, k_zero, c_sem, k_sem):
        c_zero[...] = jnp.zeros_like(c_zero)
        k_zero[...] = jnp.zeros_like(k_zero)

        def each(act):
            def block(n, _):
                r, s = n // N, n % N

                @pl.when(len_ref[r] < (s + 1) * SEQ)
                def _():
                    at = pl.ds(pl.multiple_of(s * SEQ, SEQ), SEQ)
                    act(pltpu.make_async_copy(c_zero, c_ref.at[r, at, :], c_sem.at[n]))
                    act(pltpu.make_async_copy(k_zero, k_ref.at[r, :, at], k_sem.at[n]))

                return 0

            lax.fori_loop(0, REQ * N, block, 0)

        each(lambda copy: copy.start())
        each(lambda copy: copy.wait())

    return pl.pallas_call(
        kernel,
        in_specs=[pl.BlockSpec(memory_space=pltpu.SMEM)],
        out_specs=[pl.BlockSpec(memory_space=pl.ANY)] * 2,
        out_shape=[
            jax.ShapeDtypeStruct((REQ, N * SEQ, RANK), jnp.bfloat16),
            jax.ShapeDtypeStruct((REQ, ROPE, N * SEQ), jnp.bfloat16),
        ],
        scratch_shapes=[
            pltpu.VMEM((SEQ, RANK), jnp.bfloat16),
            pltpu.VMEM((ROPE, SEQ), jnp.bfloat16),
            pltpu.SemaphoreType.DMA((REQ * N,)),
            pltpu.SemaphoreType.DMA((REQ * N,)),
        ],
        cost_estimate=pl.CostEstimate(flops=4 * 10**8, bytes_accessed=85 * 10**6, transcendentals=0),
        name="blank",
    )(lens)


def count_units(seq_lens):
    valid = jnp.clip(seq_lens[None, :] - SEQ * jnp.arange(N, dtype=jnp.int32)[:, None], 0, SEQ)
    left = valid.reshape(N, CHIPS, 2, REQ)[..., None] - UNIT * jnp.arange(PER, dtype=jnp.int32)
    left = left.transpose(0, 1, 3, 4, 2).reshape(N, CHIPS, SLOTS)
    return left


def split_place(place):
    return place // (2 * PER), place // 2 % PER, place % 2


def rank_of(have):
    places = jnp.arange(SLOTS, dtype=jnp.int32)
    return jnp.sum((have[:, None, :] & (places[None, :] <= places[:, None])).astype(jnp.int32), axis=-1)


def place_of(rank, slot):
    return jnp.sum((rank[:, None, :] <= slot[:, :, None]).astype(jnp.int32), axis=-1)


def pack_tables(me, left, slot, spill):
    have = left > 0
    places = jnp.arange(SLOTS, dtype=jnp.int32)
    chips = me // 2 ^ jnp.arange(CHIPS)
    mine = have[me][chips]
    rank = rank_of(mine)
    place = place_of(rank, slot)
    to = jnp.broadcast_to(chips[:, None], place.shape)
    if spill is not None:
        other = np.array([0, 1, 3, 2])
        spilt = spill & (place == SLOTS)
        cap = jnp.asarray(PLAN.cap)[me][:, None]
        place = jnp.where(spilt, place_of(rank[other], 2 * cap - 1 - slot), place)
        to = jnp.where(spilt, chips[other][:, None], to)
    final = jnp.max(jnp.where(mine, places, 0), axis=-1, keepdims=True)
    ok = place < SLOTS
    to = jnp.where(ok, to, chips[:, None])
    req, unit, core = split_place(jnp.where(ok, place, final))
    req = (2 * to + core) * REQ + req
    return [req.reshape(-1), unit.reshape(-1), ok.astype(jnp.int32).reshape(-1)]


def unit_codes(me, source, theirs, slot, valid):
    places = jnp.arange(SLOTS, dtype=jnp.int32)
    place = place_of(rank_of(theirs > 0), slot)
    req, unit, core = split_place(place)
    rows = jnp.sum(jnp.where(place[:, :, None] == places, theirs[:, None, :], 0), axis=-1)
    rows = jnp.where(valid & (core == me % 2), jnp.minimum(rows, UNIT), 0)
    return jnp.where(rows > 0, rows * 2**9 + req * 2**5 + source[:, None] * PER + unit, 0)


def attend_tables(me, left, slot, widths, runs, spill):
    part = jnp.arange(N)
    source = me ^ part
    chip = me // 2
    code = unit_codes(me, source, left[source, chip], slot, True)
    starts = np.cumsum([0] + list(widths))[:-1]
    inside = np.concatenate([np.arange(w) for w in widths])
    depth = np.concatenate([np.full(w, i) for run in runs for i, w in enumerate(widths[c] for c in run)])
    extra = jnp.asarray((inside * 2**18 + depth * N * 2**22).astype(np.int32))
    code = jnp.where(code > 0, code + part[:, None] * 2**22 + extra, 0)
    pieces = [code[:, s : s + w].reshape(-1) for w, s in zip(widths, starts)]
    sizes = [N * sum(widths[c] for c in run) for run in runs]
    if spill:
        source = jnp.where(chip == 3, me ^ 4, me ^ 6) ^ jnp.arange(2)
        cap = jnp.asarray(PLAN.cap[:, 2])[source][:, None]
        unused = jnp.arange(ROOM, dtype=jnp.int32)
        spilt = cap - ROOM + unused
        their_need = jnp.sum((left[source, chip ^ 1] > 0).astype(jnp.int32), axis=-1, keepdims=True)
        valid = (chip >= 2) & (spilt >= their_need)
        more = unit_codes(me, source, left[source, chip], 2 * cap - 1 - spilt, valid)
        more = jnp.where(more > 0, more + (N + jnp.arange(2))[:, None] * 2**22 + unused * 2**18, 0)
        pieces.insert(SPILL + 1, more.reshape(-1))
        sizes[SPILL] += 2 * ROOM
    code = jnp.concatenate(pieces)
    first = np.cumsum([0] + sizes)[:-1]
    run_of = np.repeat(np.arange(len(runs)), sizes).astype(np.int32)
    same = jnp.asarray(run_of)[:, None] == jnp.asarray(run_of)[None, :]
    number = jnp.arange(len(run_of), dtype=jnp.int32)
    before = jnp.sum((same & (number[None, :] < number[:, None]) & (code > 0)[None, :]).astype(jnp.int32), axis=-1)
    goes_to = jnp.where(code > 0, jnp.asarray(first[run_of].astype(np.int32)) + before, -1)
    codes = jnp.sum(jnp.where(goes_to[None, :] == number[:, None], code[None, :], 0), axis=-1)
    in_run = jnp.asarray(run_of)[None, :] == jnp.arange(len(runs), dtype=jnp.int32)[:, None]
    return codes, jnp.sum((in_run & (code > 0)[None, :]).astype(jnp.int32), axis=-1), first


def pairs(sources, hop):
    return [(s, s ^ hop) for s in sources]


def send(x, pairs):
    return lax.ppermute(x, "x", pairs)


def runs_of(count):
    return [(c,) for c in range(count - 2)] + [(count - 2, count - 1)]


def run_plan(me, left, own_lens, weights, q_lat, q_rope_t):
    plan = PLAN
    widths = [chunk[0] for chunk in plan.chunks]
    count = len(widths)
    runs = runs_of(count)
    spill = np.zeros((N, CHIPS, SLOTS), bool)
    spill[np.ix_(SPILLERS, (2, 3), range(plan.starts[SPILL], plan.starts[SPILL] + ROOM))] = True
    pack_tabs = pack_tables(me, left, jnp.asarray(plan.slot)[me], jnp.asarray(spill)[me])
    part = jnp.arange(N)
    codes, counts, first = attend_tables(me, left, jnp.asarray(plan.slot)[me ^ part, part // 2], widths, runs, True)
    caches = blank_caches(own_lens)
    landed, owns, twins = [], [], []
    after = []
    for c, (width, kind, along, across, diagonal) in enumerate(plan.chunks):
        staged = norm_pack(width, int(plan.starts[c]), SLOTS, pack_tabs, *weights, after)
        after = [staged[0]]
        sends = list(staged)
        if c >= DEPTH:
            sends, landed[c - DEPTH] = lax.optimization_barrier((sends, landed[c - DEPTH]))
        owns.append(sends[0])
        twins.append(send(sends[0], pairs(ALL, 1)))
        far = send(sends[3], pairs(ALL, 4) if kind == "relay" else pairs(diagonal, 6))
        near = send(sends[1], pairs(UP, 2) + pairs(LOW, 1) if along == UP else pairs(ALL, 2))
        over = send(sends[2], pairs(across, 4))
        landed.append([near, over, far])
    state = None
    for number, run in enumerate(runs):
        parts = []
        for c in run:
            near, over, far = landed[c]
            if plan.chunks[c][1] == "relay":
                far = send(far, pairs(LOW, 2) + pairs(UP, 1))
                far, landed[c + 1] = lax.optimization_barrier((far, landed[c + 1]))
            parts += [owns[c], twins[c]]
            for x in (near, over, far):
                parts += [x, send(x, pairs(ALL, 1))]
            if c == SPILL:
                x = send(jnp.where(me // 2 == 3, over, far), pairs(LOW, 2) + pairs(UP, 1))
                x, landed[c + 1] = lax.optimization_barrier((x, landed[c + 1]))
                parts += [x, send(x, pairs(ALL, 1))]
        got = attend(number, int(first[number]), number == 0, number == len(runs) - 1, counts, codes, parts, q_lat, q_rope_t, caches, state)
        caches, state = got[:2], got[2]
    return got


def run_extra(step, cap, me, left, weights, q_lat, q_rope_t, caches, state):
    more = step * EXTRA + jnp.arange(EXTRA, dtype=jnp.int32)
    part = jnp.arange(N)
    slot = cap[me][:, None] + more
    staged = norm_pack(EXTRA, 0, EXTRA, pack_tables(me, left, slot, None), *weights, [])
    slot = cap[me ^ part, part // 2][:, None] + more
    codes, counts, _ = attend_tables(me, left, slot, [EXTRA], [(0,)], False)
    parts = []
    for q, x in enumerate(staged):
        x = lax.ppermute(x, "x", pairs(ALL, 2 * q)) if q else x
        parts += [x, lax.ppermute(x, "x", pairs(ALL, 1))]
    return attend(0, 0, False, True, counts, codes, parts, q_lat, q_rope_t, caches, state)


def local_step(c_raw, k_raw, norm_gain, rope_cos, rope_sin, seq_lens, q_lat, q_rope):
    me = lax.axis_index("x")
    left = count_units(seq_lens)
    own_lens = lax.dynamic_slice_in_dim(seq_lens, me * REQ, REQ)
    weights = (c_raw, jnp.swapaxes(k_raw, 1, 2), norm_gain[None, :], rope_cos.T, rope_sin.T)
    q_rope_t = jnp.swapaxes(q_rope, 1, 2)
    done = run_plan(me, left, own_lens, weights, q_lat, q_rope_t)
    need = jnp.sum((left > 0).astype(jnp.int32), axis=-1)
    to = np.arange(N)[:, None] // 2 ^ np.arange(CHIPS)
    need = jnp.sum(need[:, None, :] * jnp.asarray(to[:, :, None] == np.arange(CHIPS)), axis=-1)
    spills = np.isin(np.arange(N), SPILLERS)[:, None] & np.isin(np.arange(CHIPS), (2, 3))
    room = jnp.clip(jnp.asarray(PLAN.cap) - need[:, np.array([0, 1, 3, 2])], 0, ROOM)
    cap = jnp.asarray(PLAN.cap) + jnp.where(jnp.asarray(spills), room, 0)
    steps = (jnp.maximum(jnp.max(need - cap), 0) + EXTRA - 1) // EXTRA

    def body(carry):
        step, c_cache, k_cache_t, state, _ = carry
        return step + 1, *run_extra(step, cap, me, left, weights, q_lat, q_rope_t, (c_cache, k_cache_t), state)

    _, c_cache, k_cache_t, _, o_lat = lax.while_loop(lambda carry: carry[0] < steps, body, (jnp.int32(0), *done))
    return c_cache, jnp.swapaxes(k_cache_t, 1, 2), o_lat


def solution(mesh):
    seq_spec = P("dp", "x", None)
    req_spec = P(("dp", "x"), None, None)
    return jax.shard_map(
        local_step,
        mesh=mesh,
        in_specs=(seq_spec, seq_spec, P(None), P("x", None), P("x", None), P("dp"), req_spec, req_spec),
        out_specs=(req_spec, req_spec, req_spec),
        check_vma=False,
    )
```

profile of v0, /device:TPU:0, one launch (start us, length us, event | category | flops | bytes accessed | tf_op | source)
XLA Modules:
  0.0 1409.7 jit_solution(5545783235469788219)
XLA Ops:
  11.3 6.8 norm_pack.20
  18.1 3.3 collective-permute-start.29
  21.5 11.8 norm_pack.21
  33.4 2.0 collective-permute-start.8
  38.4 73.2 %collective-permute-done.30.refs_4_ = bf16[2,1152,128]{2,1,0:T(8,128)(2,1)S(1)} collective-permute-done((bf16[2,1152,128]{2,1,0:T(8,128)(2,1)S(1)}, bf16[2,1152,128]{2,1,0:T(8,128)(2,1)S(1)}, u32[]{:S(2)}, u32[]{:S(2)}) %collective-permute-start.30) | collective-permute-done | bytes 589856 | tf_op jit(solution)/shard_map/ppermute | solution.py:425
  112.1 16.6 %norm_pack.22 = (bf16[6,1152,128]{2,1,0:T(8,128)(2,1)}, bf16[6,1152,128]{2,1,0:T(8,128)(2,1)}, bf16[6,1152,128]{2,1,0:T(8,128)(2,1)}, bf16[6,1152,128]{2,1,0:T(8,128)(2,1)}) custom-call(s32[288]{0:T(512)} %get-tuple-element.1364.req_ref, s32[288]{0:T(512)} %get-tuple-element.1363.unit_ref, s32[288]{0:T(512)} %fusion.48.ok_ref, bf16[96,768,512]{2,1,0:T(8,128)(2,1)} %c_ref.25, ...), custom_call_target="tpu_custom_call" | custom-call | flops 600000000 | bytes 14155776 | tf_op jit(solution)/shard_map/norm_pack/pallas_call | solution.py:149
  128.8 19.2 %norm_pack.23 = (bf16[7,1152,128]{2,1,0:T(8,128)(2,1)}, bf16[7,1152,128]{2,1,0:T(8,128)(2,1)}, bf16[7,1152,128]{2,1,0:T(8,128)(2,1)}, bf16[7,1152,128]{2,1,0:T(8,128)(2,1)}) custom-call(s32[288]{0:T(512)} %get-tuple-element.1364.req_ref, s32[288]{0:T(512)} %get-tuple-element.1363.unit_ref, s32[288]{0:T(512)} %fusion.48.ok_ref, bf16[96,768,512]{2,1,0:T(8,128)(2,1)} %c_ref.25, ...), custom_call_target="tpu_custom_call" | custom-call | flops 700000000 | bytes 16515072 | tf_op jit(solution)/shard_map/norm_pack/pallas_call | solution.py:149
  149.1 3.0 collective-permute-done.101.refs_7_
  153.9 2.7 collective-permute-start.34
  157.5 36.4 %collective-permute-done.32.refs_2_ = bf16[6,1152,128]{2,1,0:T(8,128)(2,1)} collective-permute-done((bf16[6,1152,128]{2,1,0:T(8,128)(2,1)}, bf16[6,1152,128]{2,1,0:T(8,128)(2,1)}, u32[]{:S(2)}, u32[]{:S(2)}) %collective-permute-start.32) | collective-permute-done | bytes 1769504 | tf_op jit(solution)/shard_map/ppermute | solution.py:425
  193.9 39.7 %collective-permute-done.33.refs_4_ = bf16[6,1152,128]{2,1,0:T(8,128)(2,1)} collective-permute-done((bf16[6,1152,128]{2,1,0:T(8,128)(2,1)}, bf16[6,1152,128]{2,1,0:T(8,128)(2,1)}, u32[]{:S(2)}, u32[]{:S(2)}) %collective-permute-start.33) | collective-permute-done | bytes 1769504 | tf_op jit(solution)/shard_map/ppermute | solution.py:425
  233.6 14.1 %norm_pack.24 = (bf16[5,1152,128]{2,1,0:T(8,128)(2,1)}, bf16[5,1152,128]{2,1,0:T(8,128)(2,1)}, bf16[5,1152,128]{2,1,0:T(8,128)(2,1)}, bf16[5,1152,128]{2,1,0:T(8,128)(2,1)}) custom-call(s32[288]{0:T(512)} %get-tuple-element.1364.req_ref, s32[288]{0:T(512)} %get-tuple-element.1363.unit_ref, s32[288]{0:T(512)} %fusion.48.ok_ref, bf16[96,768,512]{2,1,0:T(8,128)(2,1)} %c_ref.25, ...), custom_call_target="tpu_custom_call" | custom-call | flops 500000000 | bytes 11796480 | tf_op jit(solution)/shard_map/norm_pack/pallas_call | solution.py:149
  247.8 28.3 %collective-permute-done.10.refs_2_ = bf16[7,1152,128]{2,1,0:T(8,128)(2,1)} collective-permute-done((bf16[7,1152,128]{2,1,0:T(8,128)(2,1)}, bf16[7,1152,128]{2,1,0:T(8,128)(2,1)}, u32[]{:S(2)}, u32[]{:S(2)}) %collective-permute-start.10) | collective-permute-done | bytes 2064416 | tf_op jit(solution)/shard_map/ppermute | solution.py:425
  278.0 6.2 collective-permute-start.37
  284.2 69.5 %collective-permute-done.12 = bf16[7,1152,128]{2,1,0:T(8,128)(2,1)} collective-permute-done((bf16[7,1152,128]{2,1,0:T(8,128)(2,1)}, bf16[7,1152,128]{2,1,0:T(8,128)(2,1)}, u32[]{:S(2)}, u32[]{:S(2)}) %collective-permute-start.12) | collective-permute-done | bytes 2064416 | tf_op jit(solution)/shard_map/ppermute | solution.py:425
  354.3 30.5 %collective-permute-done.36.refs_4_ = bf16[5,1152,128]{2,1,0:T(8,128)(2,1)} collective-permute-done((bf16[5,1152,128]{2,1,0:T(8,128)(2,1)}, bf16[5,1152,128]{2,1,0:T(8,128)(2,1)}, u32[]{:S(2)}, u32[]{:S(2)}) %collective-permute-start.36) | collective-permute-done | bytes 1474592 | tf_op jit(solution)/shard_map/ppermute | solution.py:425
  384.8 16.6 %norm_pack.25 = (bf16[6,1152,128]{2,1,0:T(8,128)(2,1)}, bf16[6,1152,128]{2,1,0:T(8,128)(2,1)}, bf16[6,1152,128]{2,1,0:T(8,128)(2,1)}, bf16[6,1152,128]{2,1,0:T(8,128)(2,1)}) custom-call(s32[288]{0:T(512)} %get-tuple-element.1364.req_ref, s32[288]{0:T(512)} %get-tuple-element.1363.unit_ref, s32[288]{0:T(512)} %fusion.48.ok_ref, bf16[96,768,512]{2,1,0:T(8,128)(2,1)} %c_ref.25, ...), custom_call_target="tpu_custom_call" | custom-call | flops 600000000 | bytes 14155776 | tf_op jit(solution)/shard_map/norm_pack/pallas_call | solution.py:149
  402.4 2.0 collective-permute-start.15
  404.9 11.6 norm_pack.26
  416.6 26.1 %collective-permute-done.13.refs_2_ = bf16[6,1152,128]{2,1,0:T(8,128)(2,1)S(1)} collective-permute-done((bf16[6,1152,128]{2,1,0:T(8,128)(2,1)}, bf16[6,1152,128]{2,1,0:T(8,128)(2,1)S(1)}, u32[]{:S(2)}, u32[]{:S(2)}) %collective-permute-start.13) | collective-permute-done | bytes 1769504 | tf_op jit(solution)/shard_map/ppermute | solution.py:425
  444.2 37.2 %collective-permute-done.15 = bf16[6,1152,128]{2,1,0:T(8,128)(2,1)} collective-permute-done((bf16[6,1152,128]{2,1,0:T(8,128)(2,1)}, bf16[6,1152,128]{2,1,0:T(8,128)(2,1)}, u32[]{:S(2)}, u32[]{:S(2)}) %collective-permute-start.15) | collective-permute-done | bytes 1769504 | tf_op jit(solution)/shard_map/ppermute | solution.py:425
  481.4 2.2 collective-permute-start.39
  483.6 4.2 collective-permute-start.40
  487.9 49.2 %collective-permute-done.39.refs_4_ = bf16[4,1152,128]{2,1,0:T(8,128)(2,1)S(1)} collective-permute-done((bf16[4,1152,128]{2,1,0:T(8,128)(2,1)}, bf16[4,1152,128]{2,1,0:T(8,128)(2,1)S(1)}, u32[]{:S(2)}, u32[]{:S(2)}) %collective-permute-start.39) | collective-permute-done | bytes 1179680 | tf_op jit(solution)/shard_map/ppermute | solution.py:425
  538.1 24.1 %norm_pack.27 = (bf16[9,1152,128]{2,1,0:T(8,128)(2,1)}, bf16[9,1152,128]{2,1,0:T(8,128)(2,1)}, bf16[9,1152,128]{2,1,0:T(8,128)(2,1)}, bf16[9,1152,128]{2,1,0:T(8,128)(2,1)}) custom-call(s32[288]{0:T(512)} %get-tuple-element.1364.req_ref, s32[288]{0:T(512)} %get-tuple-element.1363.unit_ref, s32[288]{0:T(512)} %fusion.48.ok_ref, bf16[96,768,512]{2,1,0:T(8,128)(2,1)} %c_ref.25, ...), custom_call_target="tpu_custom_call" | custom-call | flops 900000000 | bytes 21233664 | tf_op jit(solution)/shard_map/norm_pack/pallas_call | solution.py:149
  563.4 21.6 %norm_pack.28 = (bf16[8,1152,128]{2,1,0:T(8,128)(2,1)}, bf16[8,1152,128]{2,1,0:T(8,128)(2,1)}, bf16[8,1152,128]{2,1,0:T(8,128)(2,1)}, bf16[8,1152,128]{2,1,0:T(8,128)(2,1)}) custom-call(s32[288]{0:T(512)} %get-tuple-element.1364.req_ref, s32[288]{0:T(512)} %get-tuple-element.1363.unit_ref, s32[288]{0:T(512)} %fusion.48.ok_ref, bf16[96,768,512]{2,1,0:T(8,128)(2,1)} %c_ref.25, ...), custom_call_target="tpu_custom_call" | custom-call | flops 800000000 | bytes 18874368 | tf_op jit(solution)/shard_map/norm_pack/pallas_call | solution.py:149
  585.6 10.5 collective-permute-start.43
  596.4 2.0 collective-permute-start.16
  598.4 41.1 %collective-permute-done.41.refs_2_ = bf16[8,1152,128]{2,1,0:T(8,128)(2,1)} collective-permute-done((bf16[8,1152,128]{2,1,0:T(8,128)(2,1)}, bf16[8,1152,128]{2,1,0:T(8,128)(2,1)}, u32[]{:S(2)}, u32[]{:S(2)}) %collective-permute-start.41) | collective-permute-done | bytes 2359328 | tf_op jit(solution)/shard_map/ppermute | solution.py:425
  639.4 9.7 collective-permute-start.17
  649.2 43.7 %collective-permute-start.18 = (bf16[9,1152,128]{2,1,0:T(8,128)(2,1)}, bf16[9,1152,128]{2,1,0:T(8,128)(2,1)}, u32[]{:S(2)}, u32[]{:S(2)}) collective-permute-start(bf16[9,1152,128]{2,1,0:T(8,128)(2,1)} %get-tuple-element.975), channel_id=1, source_target_pairs={{0,6},{1,7},{2,4},{4,2},{5,3},{6,0},{7,1}} | collective-permute-start | bytes 7962632 | tf_op jit(solution)/shard_map/ppermute | solution.py:425
  692.9 4.4 collective-permute-done.43.refs_6_
  697.8 48.6 %collective-permute-done.16.refs_2_ = bf16[9,1152,128]{2,1,0:T(8,128)(2,1)} collective-permute-done((bf16[9,1152,128]{2,1,0:T(8,128)(2,1)}, bf16[9,1152,128]{2,1,0:T(8,128)(2,1)}, u32[]{:S(2)}, u32[]{:S(2)}) %collective-permute-start.16) | collective-permute-done | bytes 2654240 | tf_op jit(solution)/shard_map/ppermute | solution.py:425
  746.4 4.3 collective-permute-done.17.refs_4_
  750.7 56.8 %collective-permute-done.18.refs_6_ = bf16[9,1152,128]{2,1,0:T(8,128)(2,1)} collective-permute-done((bf16[9,1152,128]{2,1,0:T(8,128)(2,1)}, bf16[9,1152,128]{2,1,0:T(8,128)(2,1)}, u32[]{:S(2)}, u32[]{:S(2)}) %collective-permute-start.18) | collective-permute-done | bytes 2654240 | tf_op jit(solution)/shard_map/ppermute | solution.py:425
  807.5 21.6 %norm_pack.29 = (bf16[8,1152,128]{2,1,0:T(8,128)(2,1)}, bf16[8,1152,128]{2,1,0:T(8,128)(2,1)}, bf16[8,1152,128]{2,1,0:T(8,128)(2,1)}, bf16[8,1152,128]{2,1,0:T(8,128)(2,1)}) custom-call(s32[288]{0:T(512)} %get-tuple-element.1364.req_ref, s32[288]{0:T(512)} %get-tuple-element.1363.unit_ref, s32[288]{0:T(512)} %fusion.48.ok_ref, bf16[96,768,512]{2,1,0:T(8,128)(2,1)} %c_ref.25, ...), custom_call_target="tpu_custom_call" | custom-call | flops 800000000 | bytes 18874368 | tf_op jit(solution)/shard_map/norm_pack/pallas_call | solution.py:149
  829.1 19.1 %norm_pack.30 = (bf16[7,1152,128]{2,1,0:T(8,128)(2,1)}, bf16[7,1152,128]{2,1,0:T(8,128)(2,1)}, bf16[7,1152,128]{2,1,0:T(8,128)(2,1)}, bf16[7,1152,128]{2,1,0:T(8,128)(2,1)}) custom-call(s32[288]{0:T(512)} %get-tuple-element.1364.req_ref, s32[288]{0:T(512)} %get-tuple-element.1363.unit_ref, s32[288]{0:T(512)} %fusion.48.ok_ref, bf16[96,768,512]{2,1,0:T(8,128)(2,1)} %c_ref.25, ...), custom_call_target="tpu_custom_call" | custom-call | flops 700000000 | bytes 16515072 | tf_op jit(solution)/shard_map/norm_pack/pallas_call | solution.py:149
  848.4 3.4 collective-permute-start.46
  854.2 42.1 %collective-permute-done.44.refs_2_ = bf16[7,1152,128]{2,1,0:T(8,128)(2,1)} collective-permute-done((bf16[7,1152,128]{2,1,0:T(8,128)(2,1)}, bf16[7,1152,128]{2,1,0:T(8,128)(2,1)}, u32[]{:S(2)}, u32[]{:S(2)}) %collective-permute-start.44) | collective-permute-done | bytes 2064416 | tf_op jit(solution)/shard_map/ppermute | solution.py:425
  896.4 42.9 %collective-permute-done.45.refs_4_ = bf16[7,1152,128]{2,1,0:T(8,128)(2,1)} collective-permute-done((bf16[7,1152,128]{2,1,0:T(8,128)(2,1)}, bf16[7,1152,128]{2,1,0:T(8,128)(2,1)}, u32[]{:S(2)}, u32[]{:S(2)}) %collective-permute-start.45) | collective-permute-done | bytes 2064416 | tf_op jit(solution)/shard_map/ppermute | solution.py:425
  942.9 19.9 %collective-permute-start.20 = (bf16[8,1152,128]{2,1,0:T(8,128)(2,1)S(1)}, bf16[8,1152,128]{2,1,0:T(8,128)(2,1)}, u32[]{:S(2)}, u32[]{:S(2)}) collective-permute-start(bf16[8,1152,128]{2,1,0:T(8,128)(2,1)S(1)} %copy-done.46), channel_id=1, source_target_pairs={{0,4},{1,5},{2,6},{3,7},{4,0},{5,1},{6,2},{7,3}} | collective-permute-start | bytes 7077896 | tf_op jit(solution)/shard_map/ppermute | solution.py:425
  963.4 30.6 %collective-permute-done.19.refs_2_ = bf16[8,1152,128]{2,1,0:T(8,128)(2,1)} collective-permute-done((bf16[8,1152,128]{2,1,0:T(8,128)(2,1)S(1)}, bf16[8,1152,128]{2,1,0:T(8,128)(2,1)}, u32[]{:S(2)}, u32[]{:S(2)}) %collective-permute-start.19) | collective-permute-done | bytes 2359328 | tf_op jit(solution)/shard_map/ppermute | solution.py:425
  994.0 64.3 %collective-permute-done.20.refs_4_ = bf16[8,1152,128]{2,1,0:T(8,128)(2,1)} collective-permute-done((bf16[8,1152,128]{2,1,0:T(8,128)(2,1)S(1)}, bf16[8,1152,128]{2,1,0:T(8,128)(2,1)}, u32[]{:S(2)}, u32[]{:S(2)}) %collective-permute-start.20) | collective-permute-done | bytes 2359328 | tf_op jit(solution)/shard_map/ppermute | solution.py:425
  1058.4 11.6 norm_pack.31
  1070.0 6.8 norm_pack.32
  1077.5 11.3 collective-permute-done.48.refs_10_
  1088.8 2.1 collective-permute-start.52
  1105.6 3.3 collective-permute-start.25
  1108.9 3.8 collective-permute-start.27
  1119.9 12.7 collective-permute-done.23.refs_2_
  1132.7 27.3 %collective-permute-done.25.refs_4_ = bf16[4,1152,128]{2,1,0:T(8,128)(2,1)} collective-permute-done((bf16[4,1152,128]{2,1,0:T(8,128)(2,1)}, bf16[4,1152,128]{2,1,0:T(8,128)(2,1)}, u32[]{:S(2)}, u32[]{:S(2)}) %collective-permute-start.25) | collective-permute-done | bytes 1179680 | tf_op jit(solution)/shard_map/ppermute | solution.py:425
  1197.3 14.9 %blank.1 = (bf16[12,6144,512]{2,1,0:T(8,128)(2,1)}, bf16[12,64,6144]{2,1,0:T(8,128)(2,1)}) custom-call(s32[12]{0:T(128)} %dynamic_slice.30.len_ref), custom_call_target="tpu_custom_call" | custom-call | flops 400000000 | bytes 85000000 | tf_op jit(solution)/shard_map/blank/pallas_call | solution.py:315
  1217.0 7.7 attend.19
  1224.8 15.5 %attend.20 = (bf16[12,6144,512]{2,1,0:T(8,128)(2,1)}, bf16[12,64,6144]{2,1,0:T(8,128)(2,1)}, f32[12,128,768]{2,1,0:T(8,128)}) custom-call(s32[12]{0:T(128)} %convert_reduce_fusion.14.count_ref, s32[592]{0:T(1024)} %select_reduce_fusion.2.code_ref, bf16[4,1152,128]{2,1,0:T(8,128)(2,1)} %get-tuple-element.938.refs_0_, ...), custom_call_target="tpu_custom_call", output_to_operand_aliasing={{0}: (12, {}), {1}: (13, {})} | custom-call | flops 200000000 | bytes 4718592 | tf_op jit(solution)/shard_map/attend/pallas_call | solution.py:274
  1240.3 21.7 %attend.21 = (bf16[12,6144,512]{2,1,0:T(8,128)(2,1)}, bf16[12,64,6144]{2,1,0:T(8,128)(2,1)}, f32[12,128,768]{2,1,0:T(8,128)}) custom-call(s32[12]{0:T(128)} %convert_reduce_fusion.14.count_ref, s32[592]{0:T(1024)} %select_reduce_fusion.2.code_ref, bf16[6,1152,128]{2,1,0:T(8,128)(2,1)} %get-tuple-element.1068.refs_0_, ...), custom_call_target="tpu_custom_call", output_to_operand_aliasing={{0}: (12, {}), {1}: (13, {})} | custom-call | flops 200000000 | bytes 4718592 | tf_op jit(solution)/shard_map/attend/pallas_call | solution.py:274
  1261.9 24.4 %attend.22 = (bf16[12,6144,512]{2,1,0:T(8,128)(2,1)}, bf16[12,64,6144]{2,1,0:T(8,128)(2,1)}, f32[12,128,768]{2,1,0:T(8,128)}) custom-call(s32[12]{0:T(128)} %convert_reduce_fusion.14.count_ref, s32[592]{0:T(1024)} %select_reduce_fusion.2.code_ref, bf16[7,1152,128]{2,1,0:T(8,128)(2,1)} %get-tuple-element.1064.refs_0_, ...), custom_call_target="tpu_custom_call", output_to_operand_aliasing={{0}: (12, {}), {1}: (13, {})} | custom-call | flops 200000000 | bytes 4718592 | tf_op jit(solution)/shard_map/attend/pallas_call | solution.py:274
  1286.3 16.2 %attend.23 = (bf16[12,6144,512]{2,1,0:T(8,128)(2,1)}, bf16[12,64,6144]{2,1,0:T(8,128)(2,1)}, f32[12,128,768]{2,1,0:T(8,128)}) custom-call(s32[12]{0:T(128)} %convert_reduce_fusion.14.count_ref, s32[592]{0:T(1024)} %select_reduce_fusion.2.code_ref, bf16[5,1152,128]{2,1,0:T(8,128)(2,1)} %get-tuple-element.1056.refs_0_, ...), custom_call_target="tpu_custom_call", output_to_operand_aliasing={{0}: (12, {}), {1}: (13, {})} | custom-call | flops 200000000 | bytes 4718592 | tf_op jit(solution)/shard_map/attend/pallas_call | solution.py:274
  1302.5 18.2 %attend.24 = (bf16[12,6144,512]{2,1,0:T(8,128)(2,1)}, bf16[12,64,6144]{2,1,0:T(8,128)(2,1)}, f32[12,128,768]{2,1,0:T(8,128)}) custom-call(s32[12]{0:T(128)} %convert_reduce_fusion.14.count_ref, s32[592]{0:T(1024)} %select_reduce_fusion.2.code_ref, bf16[6,1152,128]{2,1,0:T(8,128)(2,1)} %get-tuple-element.1052.refs_0_, ...), custom_call_target="tpu_custom_call", output_to_operand_aliasing={{0}: (12, {}), {1}: (13, {})} | custom-call | flops 200000000 | bytes 4718592 | tf_op jit(solution)/shard_map/attend/pallas_call | solution.py:274
  1320.7 15.5 %attend.25 = (bf16[12,6144,512]{2,1,0:T(8,128)(2,1)}, bf16[12,64,6144]{2,1,0:T(8,128)(2,1)}, f32[12,128,768]{2,1,0:T(8,128)}) custom-call(s32[12]{0:T(128)} %convert_reduce_fusion.14.count_ref, s32[592]{0:T(1024)} %select_reduce_fusion.2.code_ref, bf16[4,1152,128]{2,1,0:T(8,128)(2,1)} %get-tuple-element.1044.refs_0_, ...), custom_call_target="tpu_custom_call", output_to_operand_aliasing={{0}: (12, {}), {1}: (13, {})} | custom-call | flops 200000000 | bytes 4718592 | tf_op jit(solution)/shard_map/attend/pallas_call | solution.py:274
  1336.3 22.3 %attend.26 = (bf16[12,6144,512]{2,1,0:T(8,128)(2,1)}, bf16[12,64,6144]{2,1,0:T(8,128)(2,1)}, f32[12,128,768]{2,1,0:T(8,128)}) custom-call(s32[12]{0:T(128)} %convert_reduce_fusion.14.count_ref, s32[592]{0:T(1024)} %select_reduce_fusion.2.code_ref, bf16[9,1152,128]{2,1,0:T(8,128)(2,1)} %get-tuple-element.1040.refs_0_, ...), custom_call_target="tpu_custom_call", output_to_operand_aliasing={{0}: (12, {}), {1}: (13, {})} | custom-call | flops 200000000 | bytes 4718592 | tf_op jit(solution)/shard_map/attend/pallas_call | solution.py:274
  1358.6 15.5 %attend.27 = (bf16[12,6144,512]{2,1,0:T(8,128)(2,1)}, bf16[12,64,6144]{2,1,0:T(8,128)(2,1)}, f32[12,128,768]{2,1,0:T(8,128)}) custom-call(s32[12]{0:T(128)} %convert_reduce_fusion.14.count_ref, s32[592]{0:T(1024)} %select_reduce_fusion.2.code_ref, bf16[8,1152,128]{2,1,0:T(8,128)(2,1)} %get-tuple-element.1037.refs_0_, ...), custom_call_target="tpu_custom_call", output_to_operand_aliasing={{0}: (14, {}), {1}: (15, {})} | custom-call | flops 200000000 | bytes 4718592 | tf_op jit(solution)/shard_map/attend/pallas_call | solution.py:274
  1374.1 14.1 %attend.28 = (bf16[12,6144,512]{2,1,0:T(8,128)(2,1)}, bf16[12,64,6144]{2,1,0:T(8,128)(2,1)}, f32[12,128,768]{2,1,0:T(8,128)}) custom-call(s32[12]{0:T(128)} %convert_reduce_fusion.14.count_ref, s32[592]{0:T(1024)} %select_reduce_fusion.2.code_ref, bf16[8,1152,128]{2,1,0:T(8,128)(2,1)} %get-tuple-element.1028.refs_0_, ...), custom_call_target="tpu_custom_call", output_to_operand_aliasing={{0}: (12, {}), {1}: (13, {})} | custom-call | flops 200000000 | bytes 4718592 | tf_op jit(solution)/shard_map/attend/pallas_call | solution.py:274
  1388.3 10.7 attend.29
  1399.1 10.3 attend.30
  (363 shorter events, 97.6 us)
Async XLA Ops:
  33.3 95.5 %collective-permute-start.7 = (bf16[4,1152,128]{2,1,0:T(8,128)(2,1)}, bf16[4,1152,128]{2,1,0:T(8,128)(2,1)}, u32[]{:S(2)}, u32[]{:S(2)}) collective-permute-start(bf16[4,1152,128]{2,1,0:T(8,128)(2,1)} %get-tuple-element.964), channel_id=1, source_target_pairs={{0,2},{1,3},{2,0},{3,1},{4,6},{5,7},{6,4},{7,5}} | collective-permute-start | bytes 3538952 | tf_op jit(solution)/shard_map/ppermute | solution.py:425
  33.4 114.7 %collective-permute-start.8 = (bf16[4,1152,128]{2,1,0:T(8,128)(2,1)}, bf16[4,1152,128]{2,1,0:T(8,128)(2,1)}, u32[]{:S(2)}, u32[]{:S(2)}) collective-permute-start(bf16[4,1152,128]{2,1,0:T(8,128)(2,1)} %get-tuple-element.965), channel_id=1, source_target_pairs={{0,4},{1,5},{2,6},{3,7},{4,0},{5,1},{6,2},{7,3}} | collective-permute-start | bytes 3538952 | tf_op jit(solution)/shard_map/ppermute | solution.py:425
  35.4 112.7 %collective-permute-start.9 = (bf16[4,1152,128]{2,1,0:T(8,128)(2,1)}, bf16[4,1152,128]{2,1,0:T(8,128)(2,1)}, u32[]{:S(2)}, u32[]{:S(2)}) collective-permute-start(bf16[4,1152,128]{2,1,0:T(8,128)(2,1)} %get-tuple-element.966), channel_id=1, source_target_pairs={{0,6},{1,7},{2,4},{3,5},{4,2},{5,3},{6,0},{7,1}} | collective-permute-start | bytes 3538952 | tf_op jit(solution)/shard_map/ppermute | solution.py:425
  36.8 74.8 %collective-permute-start.30 = (bf16[2,1152,128]{2,1,0:T(8,128)(2,1)S(1)}, bf16[2,1152,128]{2,1,0:T(8,128)(2,1)S(1)}, u32[]{:S(2)}, u32[]{:S(2)}) collective-permute-start(bf16[2,1152,128]{2,1,0:T(8,128)(2,1)S(1)} %copy-done.49), channel_id=1, source_target_pairs={{0,4},{1,5},{2,6},{3,7},{4,0},{5,1},{6,2},{7,3}} | collective-permute-start | bytes 1769480 | tf_op jit(solution)/shard_map/ppermute | solution.py:425
  38.3 73.2 %collective-permute-start.31 = (bf16[2,1152,128]{2,1,0:T(8,128)(2,1)S(1)}, bf16[2,1152,128]{2,1,0:T(8,128)(2,1)}, u32[]{:S(2)}, u32[]{:S(2)}) collective-permute-start(bf16[2,1152,128]{2,1,0:T(8,128)(2,1)S(1)} %copy-done.48), channel_id=1, source_target_pairs={{0,6},{1,7},{2,4},{3,5},{4,2},{5,3},{6,0},{7,1}} | collective-permute-start | bytes 1769480 | tf_op jit(solution)/shard_map/ppermute | solution.py:425
  111.6 42.3 %collective-permute-start.94 = (bf16[4,1152,128]{2,1,0:T(8,128)(2,1)}, bf16[4,1152,128]{2,1,0:T(8,128)(2,1)}, u32[]{:S(2)}, u32[]{:S(2)}) collective-permute-start(bf16[4,1152,128]{2,1,0:T(8,128)(2,1)} %get-tuple-element.938.refs_0_), channel_id=1, source_target_pairs={{0,1},{1,0},{2,3},{3,2},{4,5},{5,4},{6,7},{7,6}} | collective-permute-start | bytes 3538952 | tf_op jit(solution)/shard_map/ppermute | solution.py:425
  153.9 79.7 %collective-permute-start.33 = (bf16[6,1152,128]{2,1,0:T(8,128)(2,1)}, bf16[6,1152,128]{2,1,0:T(8,128)(2,1)}, u32[]{:S(2)}, u32[]{:S(2)}) collective-permute-start(bf16[6,1152,128]{2,1,0:T(8,128)(2,1)} %get-tuple-element.1006), channel_id=1, source_target_pairs={{0,4},{1,5},{2,6},{3,7},{4,0},{5,1},{6,2},{7,3}} | collective-permute-start | bytes 5308424 | tf_op jit(solution)/shard_map/ppermute | solution.py:425
  153.9 79.7 %collective-permute-start.34 = (bf16[6,1152,128]{2,1,0:T(8,128)(2,1)}, bf16[6,1152,128]{2,1,0:T(8,128)(2,1)}, u32[]{:S(2)}, u32[]{:S(2)}) collective-permute-start(bf16[6,1152,128]{2,1,0:T(8,128)(2,1)} %get-tuple-element.1007), channel_id=1, source_target_pairs={{0,6},{1,7},{2,4},{3,5},{4,2},{5,3},{6,0},{7,1}} | collective-permute-start | bytes 5308424 | tf_op jit(solution)/shard_map/ppermute | solution.py:425
  156.6 119.5 %collective-permute-start.10 = (bf16[7,1152,128]{2,1,0:T(8,128)(2,1)}, bf16[7,1152,128]{2,1,0:T(8,128)(2,1)}, u32[]{:S(2)}, u32[]{:S(2)}) collective-permute-start(bf16[7,1152,128]{2,1,0:T(8,128)(2,1)} %get-tuple-element.967), channel_id=1, source_target_pairs={{0,2},{1,3},{2,0},{3,1},{4,5},{5,4},{6,7},{7,6}} | collective-permute-start | bytes 6193160 | tf_op jit(solution)/shard_map/ppermute | solution.py:425
  157.4 90.4 %collective-permute-start.90 = (bf16[6,1152,128]{2,1,0:T(8,128)(2,1)S(1)}, bf16[6,1152,128]{2,1,0:T(8,128)(2,1)}, u32[]{:S(2)}, u32[]{:S(2)}) collective-permute-start(bf16[6,1152,128]{2,1,0:T(8,128)(2,1)S(1)} %copy-done.8), channel_id=1, source_target_pairs={{0,1},{1,0},{2,3},{3,2},{4,5},{5,4},{6,7},{7,6}} | collective-permute-start | bytes 5308424 | tf_op jit(solution)/shard_map/ppermute | solution.py:425
  193.9 84.1 %collective-permute-start.11 = (bf16[7,1152,128]{2,1,0:T(8,128)(2,1)}, bf16[7,1152,128]{2,1,0:T(8,128)(2,1)}, u32[]{:S(2)}, u32[]{:S(2)}) collective-permute-start(bf16[7,1152,128]{2,1,0:T(8,128)(2,1)} %get-tuple-element.968), channel_id=1, source_target_pairs={{0,4},{1,5},{2,6},{3,7},{4,0},{5,1},{6,2},{7,3}} | collective-permute-start | bytes 6193160 | tf_op jit(solution)/shard_map/ppermute | solution.py:425
  233.6 120.1 %collective-permute-start.12 = (bf16[7,1152,128]{2,1,0:T(8,128)(2,1)}, bf16[7,1152,128]{2,1,0:T(8,128)(2,1)}, u32[]{:S(2)}, u32[]{:S(2)}) collective-permute-start(bf16[7,1152,128]{2,1,0:T(8,128)(2,1)} %get-tuple-element.969), channel_id=1, source_target_pairs={{0,4},{1,5},{2,6},{3,7},{4,0},{5,1},{6,2},{7,3}} | collective-permute-start | bytes 6193160 | tf_op jit(solution)/shard_map/ppermute | solution.py:425
  233.6 120.1 %collective-permute-start.86 = (bf16[7,1152,128]{2,1,0:T(8,128)(2,1)}, bf16[7,1152,128]{2,1,0:T(8,128)(2,1)}, u32[]{:S(2)}, u32[]{:S(2)}) collective-permute-start(bf16[7,1152,128]{2,1,0:T(8,128)(2,1)} %get-tuple-element.1064.refs_0_), channel_id=1, source_target_pairs={{0,1},{1,0},{2,3},{3,2},{4,5},{5,4},{6,7},{7,6}} | collective-permute-start | bytes 6193160 | tf_op jit(solution)/shard_map/ppermute | solution.py:425
  247.8 106.4 %collective-permute-start.35 = (bf16[5,1152,128]{2,1,0:T(8,128)(2,1)}, bf16[5,1152,128]{2,1,0:T(8,128)(2,1)S(1)}, u32[]{:S(2)}, u32[]{:S(2)}) collective-permute-start(bf16[5,1152,128]{2,1,0:T(8,128)(2,1)} %get-tuple-element.1008), channel_id=1, source_target_pairs={{0,2},{1,3},{2,0},{3,1},{4,6},{5,7},{6,4},{7,5}} | collective-permute-start | bytes 4423688 | tf_op jit(solution)/shard_map/ppermute | solution.py:425
  276.1 108.7 %collective-permute-start.36 = (bf16[5,1152,128]{2,1,0:T(8,128)(2,1)}, bf16[5,1152,128]{2,1,0:T(8,128)(2,1)}, u32[]{:S(2)}, u32[]{:S(2)}) collective-permute-start(bf16[5,1152,128]{2,1,0:T(8,128)(2,1)} %get-tuple-element.1009), channel_id=1, source_target_pairs={{0,4},{1,5},{4,0},{5,1},{6,2},{7,3}} | collective-permute-start | bytes 4423688 | tf_op jit(solution)/shard_map/ppermute | solution.py:425
  278.0 123.4 %collective-permute-start.37 = (bf16[5,1152,128]{2,1,0:T(8,128)(2,1)}, bf16[5,1152,128]{2,1,0:T(8,128)(2,1)}, u32[]{:S(2)}, u32[]{:S(2)}) collective-permute-start(bf16[5,1152,128]{2,1,0:T(8,128)(2,1)} %get-tuple-element.1010), channel_id=1, source_target_pairs={{0,6},{1,7},{4,2},{5,3},{6,0},{7,1}} | collective-permute-start | bytes 4423688 | tf_op jit(solution)/shard_map/ppermute | solution.py:425
  353.7 48.7 %collective-permute-start.91 = (bf16[6,1152,128]{2,1,0:T(8,128)(2,1)}, bf16[6,1152,128]{2,1,0:T(8,128)(2,1)}, u32[]{:S(2)}, u32[]{:S(2)}) collective-permute-start(bf16[6,1152,128]{2,1,0:T(8,128)(2,1)} %collective-permute-done.32.refs_2_), channel_id=1, source_target_pairs={{0,1},{1,0},{2,3},{3,2},{4,5},{5,4},{6,7},{7,6}} | collective-permute-start | bytes 5308424 | tf_op jit(solution)/shard_map/ppermute | solution.py:425
  353.7 48.7 %collective-permute-start.81 = (bf16[5,1152,128]{2,1,0:T(8,128)(2,1)}, bf16[5,1152,128]{2,1,0:T(8,128)(2,1)}, u32[]{:S(2)}, u32[]{:S(2)}) collective-permute-start(bf16[5,1152,128]{2,1,0:T(8,128)(2,1)} %get-tuple-element.1056.refs_0_), channel_id=1, source_target_pairs={{0,1},{1,0},{2,3},{3,2},{4,5},{5,4},{6,7},{7,6}} | collective-permute-start | bytes 4423688 | tf_op jit(solution)/shard_map/ppermute | solution.py:425
  354.2 50.2 %collective-permute-start.92 = (bf16[6,1152,128]{2,1,0:T(8,128)(2,1)}, bf16[6,1152,128]{2,1,0:T(8,128)(2,1)}, u32[]{:S(2)}, u32[]{:S(2)}) collective-permute-start(bf16[6,1152,128]{2,1,0:T(8,128)(2,1)} %collective-permute-done.33.refs_4_), channel_id=1, source_target_pairs={{0,1},{1,0},{2,3},{3,2},{4,5},{5,4},{6,7},{7,6}} | collective-permute-start | bytes 5308424 | tf_op jit(solution)/shard_map/ppermute | solution.py:425
  402.4 41.8 %collective-permute-start.14 = (bf16[6,1152,128]{2,1,0:T(8,128)(2,1)}, bf16[6,1152,128]{2,1,0:T(8,128)(2,1)}, u32[]{:S(2)}, u32[]{:S(2)}) collective-permute-start(bf16[6,1152,128]{2,1,0:T(8,128)(2,1)} %get-tuple-element.971), channel_id=1, source_target_pairs={{0,4},{1,5},{2,6},{3,7},{4,0},{5,1},{6,2},{7,3}} | collective-permute-start | bytes 5308424 | tf_op jit(solution)/shard_map/ppermute | solution.py:425
  402.4 79.0 %collective-permute-start.15 = (bf16[6,1152,128]{2,1,0:T(8,128)(2,1)}, bf16[6,1152,128]{2,1,0:T(8,128)(2,1)}, u32[]{:S(2)}, u32[]{:S(2)}) collective-permute-start(bf16[6,1152,128]{2,1,0:T(8,128)(2,1)} %get-tuple-element.972), channel_id=1, source_target_pairs={{0,4},{1,5},{2,6},{3,7},{4,0},{5,1},{6,2},{7,3}} | collective-permute-start | bytes 5308424 | tf_op jit(solution)/shard_map/ppermute | solution.py:425
  404.4 83.4 %collective-permute-start.82 = (bf16[7,1152,128]{2,1,0:T(8,128)(2,1)}, bf16[7,1152,128]{2,1,0:T(8,128)(2,1)}, u32[]{:S(2)}, u32[]{:S(2)}) collective-permute-start(bf16[7,1152,128]{2,1,0:T(8,128)(2,1)} %collective-permute-done.12), channel_id=1, source_target_pairs={{4,6},{5,7},{6,4},{7,5},{0,1},{1,0},{2,3},{3,2}} | collective-permute-start | bytes 6193160 | tf_op jit(solution)/shard_map/ppermute | solution.py:425
  404.4 76.9 %collective-permute-start.77 = (bf16[6,1152,128]{2,1,0:T(8,128)(2,1)}, bf16[6,1152,128]{2,1,0:T(8,128)(2,1)}, u32[]{:S(2)}, u32[]{:S(2)}) collective-permute-start(bf16[6,1152,128]{2,1,0:T(8,128)(2,1)} %get-tuple-element.1052.refs_0_), channel_id=1, source_target_pairs={{0,1},{1,0},{2,3},{3,2},{4,5},{5,4},{6,7},{7,6}} | collective-permute-start | bytes 5308424 | tf_op jit(solution)/shard_map/ppermute | solution.py:425
  444.2 118.7 %collective-permute-start.87 = (bf16[7,1152,128]{2,1,0:T(8,128)(2,1)}, bf16[7,1152,128]{2,1,0:T(8,128)(2,1)}, u32[]{:S(2)}, u32[]{:S(2)}) collective-permute-start(bf16[7,1152,128]{2,1,0:T(8,128)(2,1)} %collective-permute-done.10.refs_2_), channel_id=1, source_target_pairs={{0,1},{1,0},{2,3},{3,2},{4,5},{5,4},{6,7},{7,6}} | collective-permute-start | bytes 6193160 | tf_op jit(solution)/shard_map/ppermute | solution.py:425
  481.4 82.0 %collective-permute-start.88 = (bf16[7,1152,128]{2,1,0:T(8,128)(2,1)}, bf16[7,1152,128]{2,1,0:T(8,128)(2,1)}, u32[]{:S(2)}, u32[]{:S(2)}) collective-permute-start(bf16[7,1152,128]{2,1,0:T(8,128)(2,1)} %collective-permute-done.11.refs_4_), channel_id=1, source_target_pairs={{0,1},{1,0},{2,3},{3,2},{4,5},{5,4},{6,7},{7,6}} | collective-permute-start | bytes 6193160 | tf_op jit(solution)/shard_map/ppermute | solution.py:425
  481.4 55.8 %collective-permute-start.39 = (bf16[4,1152,128]{2,1,0:T(8,128)(2,1)}, bf16[4,1152,128]{2,1,0:T(8,128)(2,1)S(1)}, u32[]{:S(2)}, u32[]{:S(2)}) collective-permute-start(bf16[4,1152,128]{2,1,0:T(8,128)(2,1)} %get-tuple-element.1012), channel_id=1, source_target_pairs={{0,4},{1,5},{4,0},{5,1},{6,2},{7,3}} | collective-permute-start | bytes 3538952 | tf_op jit(solution)/shard_map/ppermute | solution.py:425
  483.6 78.7 %collective-permute-start.40 = (bf16[4,1152,128]{2,1,0:T(8,128)(2,1)}, bf16[4,1152,128]{2,1,0:T(8,128)(2,1)}, u32[]{:S(2)}, u32[]{:S(2)}) collective-permute-start(bf16[4,1152,128]{2,1,0:T(8,128)(2,1)} %get-tuple-element.1013), channel_id=1, source_target_pairs={{0,6},{1,7},{4,2},{5,3},{6,0},{7,1}} | collective-permute-start | bytes 3538952 | tf_op jit(solution)/shard_map/ppermute | solution.py:425
  487.8 75.0 %collective-permute-start.72 = (bf16[4,1152,128]{2,1,0:T(8,128)(2,1)}, bf16[4,1152,128]{2,1,0:T(8,128)(2,1)}, u32[]{:S(2)}, u32[]{:S(2)}) collective-permute-start(bf16[4,1152,128]{2,1,0:T(8,128)(2,1)} %get-tuple-element.1044.refs_0_), channel_id=1, source_target_pairs={{0,1},{1,0},{2,3},{3,2},{4,5},{5,4},{6,7},{7,6}} | collective-permute-start | bytes 3538952 | tf_op jit(solution)/shard_map/ppermute | solution.py:425
  538.1 46.8 %collective-permute-start.83 = (bf16[5,1152,128]{2,1,0:T(8,128)(2,1)S(1)}, bf16[5,1152,128]{2,1,0:T(8,128)(2,1)}, u32[]{:S(2)}, u32[]{:S(2)}) collective-permute-start(bf16[5,1152,128]{2,1,0:T(8,128)(2,1)S(1)} %collective-permute-done.35.refs_2_), channel_id=1, source_target_pairs={{0,1},{1,0},{2,3},{3,2},{4,5},{5,4},{6,7},{7,6}} | collective-permute-start | bytes 4423688 | tf_op jit(solution)/shard_map/ppermute | solution.py:425
  585.0 54.5 %collective-permute-start.41 = (bf16[8,1152,128]{2,1,0:T(8,128)(2,1)}, bf16[8,1152,128]{2,1,0:T(8,128)(2,1)}, u32[]{:S(2)}, u32[]{:S(2)}) collective-permute-start(bf16[8,1152,128]{2,1,0:T(8,128)(2,1)} %get-tuple-element.1014), channel_id=1, source_target_pairs={{0,2},{1,3},{2,0},{3,1},{4,6},{5,7},{6,4},{7,5}} | collective-permute-start | bytes 7077896 | tf_op jit(solution)/shard_map/ppermute | solution.py:425
  585.0 64.1 %collective-permute-start.42 = (bf16[8,1152,128]{2,1,0:T(8,128)(2,1)}, bf16[8,1152,128]{2,1,0:T(8,128)(2,1)}, u32[]{:S(2)}, u32[]{:S(2)}) collective-permute-start(bf16[8,1152,128]{2,1,0:T(8,128)(2,1)} %get-tuple-element.1015), channel_id=1, source_target_pairs={{0,4},{1,5},{2,6},{3,7},{4,0},{5,1},{6,2},{7,3}} | collective-permute-start | bytes 7077896 | tf_op jit(solution)/shard_map/ppermute | solution.py:425
  585.6 111.7 %collective-permute-start.43 = (bf16[8,1152,128]{2,1,0:T(8,128)(2,1)}, bf16[8,1152,128]{2,1,0:T(8,128)(2,1)}, u32[]{:S(2)}, u32[]{:S(2)}) collective-permute-start(bf16[8,1152,128]{2,1,0:T(8,128)(2,1)} %get-tuple-element.1016), channel_id=1, source_target_pairs={{0,6},{1,7},{2,4},{3,5},{4,2},{5,3},{6,0},{7,1}} | collective-permute-start | bytes 7077896 | tf_op jit(solution)/shard_map/ppermute | solution.py:425
  596.1 101.1 %collective-permute-start.63 = (bf16[8,1152,128]{2,1,0:T(8,128)(2,1)}, bf16[8,1152,128]{2,1,0:T(8,128)(2,1)}, u32[]{:S(2)}, u32[]{:S(2)}) collective-permute-start(bf16[8,1152,128]{2,1,0:T(8,128)(2,1)} %get-tuple-element.1037.refs_0_), channel_id=1, source_target_pairs={{0,1},{1,0},{2,3},{3,2},{4,5},{5,4},{6,7},{7,6}} | collective-permute-start | bytes 7077896 | tf_op jit(solution)/shard_map/ppermute | solution.py:425
  596.4 150.1 %collective-permute-start.16 = (bf16[9,1152,128]{2,1,0:T(8,128)(2,1)}, bf16[9,1152,128]{2,1,0:T(8,128)(2,1)}, u32[]{:S(2)}, u32[]{:S(2)}) collective-permute-start(bf16[9,1152,128]{2,1,0:T(8,128)(2,1)} %get-tuple-element.973), channel_id=1, source_target_pairs={{0,2},{1,3},{2,0},{3,1},{4,6},{5,7},{6,4},{7,5}} | collective-permute-start | bytes 7962632 | tf_op jit(solution)/shard_map/ppermute | solution.py:425
  639.4 111.3 %collective-permute-start.17 = (bf16[9,1152,128]{2,1,0:T(8,128)(2,1)}, bf16[9,1152,128]{2,1,0:T(8,128)(2,1)}, u32[]{:S(2)}, u32[]{:S(2)}) collective-permute-start(bf16[9,1152,128]{2,1,0:T(8,128)(2,1)} %get-tuple-element.974), channel_id=1, source_target_pairs={{0,4},{1,5},{2,6},{4,0},{5,1},{6,2},{7,3}} | collective-permute-start | bytes 7962632 | tf_op jit(solution)/shard_map/ppermute | solution.py:425
  649.2 158.3 %collective-permute-start.18 = (bf16[9,1152,128]{2,1,0:T(8,128)(2,1)}, bf16[9,1152,128]{2,1,0:T(8,128)(2,1)}, u32[]{:S(2)}, u32[]{:S(2)}) collective-permute-start(bf16[9,1152,128]{2,1,0:T(8,128)(2,1)} %get-tuple-element.975), channel_id=1, source_target_pairs={{0,6},{1,7},{2,4},{4,2},{5,3},{6,0},{7,1}} | collective-permute-start | bytes 7962632 | tf_op jit(solution)/shard_map/ppermute | solution.py:425
  697.3 150.9 %collective-permute-start.68 = (bf16[9,1152,128]{2,1,0:T(8,128)(2,1)}, bf16[9,1152,128]{2,1,0:T(8,128)(2,1)}, u32[]{:S(2)}, u32[]{:S(2)}) collective-permute-start(bf16[9,1152,128]{2,1,0:T(8,128)(2,1)} %get-tuple-element.1040.refs_0_), channel_id=1, source_target_pairs={{0,1},{1,0},{2,3},{3,2},{4,5},{5,4},{6,7},{7,6}} | collective-permute-start | bytes 7962632 | tf_op jit(solution)/shard_map/ppermute | solution.py:425
  697.3 151.0 %collective-permute-start.74 = (bf16[4,1152,128]{2,1,0:T(8,128)(2,1)}, bf16[4,1152,128]{2,1,0:T(8,128)(2,1)S(1)}, u32[]{:S(2)}, u32[]{:S(2)}) collective-permute-start(bf16[4,1152,128]{2,1,0:T(8,128)(2,1)} %copy-done.19), channel_id=1, source_target_pairs={{0,1},{1,0},{2,3},{3,2},{4,5},{5,4},{6,7},{7,6}} | collective-permute-start | bytes 3538952 | tf_op jit(solution)/shard_map/ppermute | solution.py:425
  746.4 101.9 %collective-permute-start.75 = (bf16[4,1152,128]{2,1,0:T(8,128)(2,1)}, bf16[4,1152,128]{2,1,0:T(8,128)(2,1)}, u32[]{:S(2)}, u32[]{:S(2)}) collective-permute-start(bf16[4,1152,128]{2,1,0:T(8,128)(2,1)} %copy-done.20), channel_id=1, source_target_pairs={{0,1},{1,0},{2,3},{3,2},{4,5},{5,4},{6,7},{7,6}} | collective-permute-start | bytes 3538952 | tf_op jit(solution)/shard_map/ppermute | solution.py:425
  750.7 101.0 %collective-permute-start.76 = (bf16[4,1152,128]{2,1,0:T(8,128)(2,1)}, bf16[4,1152,128]{2,1,0:T(8,128)(2,1)}, u32[]{:S(2)}, u32[]{:S(2)}) collective-permute-start(bf16[4,1152,128]{2,1,0:T(8,128)(2,1)} %collective-permute-done.40.refs_6_), channel_id=1, source_target_pairs={{0,1},{1,0},{2,3},{3,2},{4,5},{5,4},{6,7},{7,6}} | collective-permute-start | bytes 3538952 | tf_op jit(solution)/shard_map/ppermute | solution.py:425
  807.5 46.2 %collective-permute-start.80 = (bf16[6,1152,128]{2,1,0:T(8,128)(2,1)}, bf16[6,1152,128]{2,1,0:T(8,128)(2,1)S(1)}, u32[]{:S(2)}, u32[]{:S(2)}) collective-permute-start(bf16[6,1152,128]{2,1,0:T(8,128)(2,1)} %collective-permute-done.73.refs_6_), channel_id=1, source_target_pairs={{0,1},{1,0},{2,3},{3,2},{4,5},{5,4},{6,7},{7,6}} | collective-permute-start | bytes 5308424 | tf_op jit(solution)/shard_map/ppermute | solution.py:425
  848.2 48.1 %collective-permute-start.44 = (bf16[7,1152,128]{2,1,0:T(8,128)(2,1)}, bf16[7,1152,128]{2,1,0:T(8,128)(2,1)}, u32[]{:S(2)}, u32[]{:S(2)}) collective-permute-start(bf16[7,1152,128]{2,1,0:T(8,128)(2,1)} %get-tuple-element.1017), channel_id=1, source_target_pairs={{0,2},{1,3},{2,0},{3,1},{4,6},{5,7},{6,4},{7,5}} | collective-permute-start | bytes 6193160 | tf_op jit(solution)/shard_map/ppermute | solution.py:425
  848.3 91.0 %collective-permute-start.45 = (bf16[7,1152,128]{2,1,0:T(8,128)(2,1)}, bf16[7,1152,128]{2,1,0:T(8,128)(2,1)}, u32[]{:S(2)}, u32[]{:S(2)}) collective-permute-start(bf16[7,1152,128]{2,1,0:T(8,128)(2,1)} %get-tuple-element.1018), channel_id=1, source_target_pairs={{0,4},{1,5},{2,6},{3,7},{4,0},{5,1},{6,2},{7,3}} | collective-permute-start | bytes 6193160 | tf_op jit(solution)/shard_map/ppermute | solution.py:425
  848.4 90.9 %collective-permute-start.46 = (bf16[7,1152,128]{2,1,0:T(8,128)(2,1)}, bf16[7,1152,128]{2,1,0:T(8,128)(2,1)S(1)}, u32[]{:S(2)}, u32[]{:S(2)}) collective-permute-start(bf16[7,1152,128]{2,1,0:T(8,128)(2,1)} %get-tuple-element.1019), channel_id=1, source_target_pairs={{0,6},{1,7},{2,4},{3,5},{4,2},{5,3},{6,0},{7,1}} | collective-permute-start | bytes 6193160 | tf_op jit(solution)/shard_map/ppermute | solution.py:425
  851.8 88.0 %collective-permute-start.54 = (bf16[7,1152,128]{2,1,0:T(8,128)(2,1)}, bf16[7,1152,128]{2,1,0:T(8,128)(2,1)S(1)}, u32[]{:S(2)}, u32[]{:S(2)}) collective-permute-start(bf16[7,1152,128]{2,1,0:T(8,128)(2,1)} %get-tuple-element.1024.refs_0_), channel_id=1, source_target_pairs={{0,1},{1,0},{2,3},{3,2},{4,5},{5,4},{6,7},{7,6}} | collective-permute-start | bytes 6193160 | tf_op jit(solution)/shard_map/ppermute | solution.py:425
  853.7 87.8 %collective-permute-start.59 = (bf16[8,1152,128]{2,1,0:T(8,128)(2,1)S(1)}, bf16[8,1152,128]{2,1,0:T(8,128)(2,1)S(1)}, u32[]{:S(2)}, u32[]{:S(2)}) collective-permute-start(bf16[8,1152,128]{2,1,0:T(8,128)(2,1)S(1)} %broadcast_select_fusion.1), channel_id=1, source_target_pairs={{4,6},{5,7},{6,4},{7,5},{0,1},{1,0},{2,3},{3,2}} | collective-permute-start | bytes 7077896 | tf_op jit(solution)/shard_map/ppermute | solution.py:425
  896.4 66.4 %collective-permute-start.64 = (bf16[8,1152,128]{2,1,0:T(8,128)(2,1)}, bf16[8,1152,128]{2,1,0:T(8,128)(2,1)}, u32[]{:S(2)}, u32[]{:S(2)}) collective-permute-start(bf16[8,1152,128]{2,1,0:T(8,128)(2,1)} %collective-permute-done.41.refs_2_), channel_id=1, source_target_pairs={{0,1},{1,0},{2,3},{3,2},{4,5},{5,4},{6,7},{7,6}} | collective-permute-start | bytes 7077896 | tf_op jit(solution)/shard_map/ppermute | solution.py:425
  939.8 54.2 %collective-permute-start.19 = (bf16[8,1152,128]{2,1,0:T(8,128)(2,1)S(1)}, bf16[8,1152,128]{2,1,0:T(8,128)(2,1)}, u32[]{:S(2)}, u32[]{:S(2)}) collective-permute-start(bf16[8,1152,128]{2,1,0:T(8,128)(2,1)S(1)} %copy-done.47), channel_id=1, source_target_pairs={{0,2},{1,3},{2,0},{3,1},{4,6},{5,7},{6,4},{7,5}} | collective-permute-start | bytes 7077896 | tf_op jit(solution)/shard_map/ppermute | solution.py:425
  942.9 115.4 %collective-permute-start.20 = (bf16[8,1152,128]{2,1,0:T(8,128)(2,1)S(1)}, bf16[8,1152,128]{2,1,0:T(8,128)(2,1)}, u32[]{:S(2)}, u32[]{:S(2)}) collective-permute-start(bf16[8,1152,128]{2,1,0:T(8,128)(2,1)S(1)} %copy-done.46), channel_id=1, source_target_pairs={{0,4},{1,5},{2,6},{3,7},{4,0},{5,1},{6,2},{7,3}} | collective-permute-start | bytes 7077896 | tf_op jit(solution)/shard_map/ppermute | solution.py:425
  962.8 114.0 %collective-permute-start.21 = (bf16[8,1152,128]{2,1,0:T(8,128)(2,1)}, bf16[8,1152,128]{2,1,0:T(8,128)(2,1)}, u32[]{:S(2)}, u32[]{:S(2)}) collective-permute-start(bf16[8,1152,128]{2,1,0:T(8,128)(2,1)} %get-tuple-element.978), channel_id=1, source_target_pairs={{0,6},{1,7},{2,4},{3,5},{4,2},{5,3},{6,0},{7,1}} | collective-permute-start | bytes 7077896 | tf_op jit(solution)/shard_map/ppermute | solution.py:425
  962.8 114.0 %collective-permute-start.58 = (bf16[8,1152,128]{2,1,0:T(8,128)(2,1)}, bf16[8,1152,128]{2,1,0:T(8,128)(2,1)}, u32[]{:S(2)}, u32[]{:S(2)}) collective-permute-start(bf16[8,1152,128]{2,1,0:T(8,128)(2,1)} %get-tuple-element.1028.refs_0_), channel_id=1, source_target_pairs={{0,1},{1,0},{2,3},{3,2},{4,5},{5,4},{6,7},{7,6}} | collective-permute-start | bytes 7077896 | tf_op jit(solution)/shard_map/ppermute | solution.py:425
  962.9 138.1 %collective-permute-start.69 = (bf16[9,1152,128]{2,1,0:T(8,128)(2,1)}, bf16[9,1152,128]{2,1,0:T(8,128)(2,1)}, u32[]{:S(2)}, u32[]{:S(2)}) collective-permute-start(bf16[9,1152,128]{2,1,0:T(8,128)(2,1)} %collective-permute-done.16.refs_2_), channel_id=1, source_target_pairs={{0,1},{1,0},{2,3},{3,2},{4,5},{5,4},{6,7},{7,6}} | collective-permute-start | bytes 7962632 | tf_op jit(solution)/shard_map/ppermute | solution.py:425
  994.0 107.6 %collective-permute-start.70 = (bf16[9,1152,128]{2,1,0:T(8,128)(2,1)}, bf16[9,1152,128]{2,1,0:T(8,128)(2,1)}, u32[]{:S(2)}, u32[]{:S(2)}) collective-permute-start(bf16[9,1152,128]{2,1,0:T(8,128)(2,1)} %collective-permute-done.17.refs_4_), channel_id=1, source_target_pairs={{0,1},{1,0},{2,3},{3,2},{4,5},{5,4},{6,7},{7,6}} | collective-permute-start | bytes 7962632 | tf_op jit(solution)/shard_map/ppermute | solution.py:425
  1058.4 45.2 %collective-permute-start.71 = (bf16[9,1152,128]{2,1,0:T(8,128)(2,1)}, bf16[9,1152,128]{2,1,0:T(8,128)(2,1)}, u32[]{:S(2)}, u32[]{:S(2)}) collective-permute-start(bf16[9,1152,128]{2,1,0:T(8,128)(2,1)} %collective-permute-done.18.refs_6_), channel_id=1, source_target_pairs={{0,1},{1,0},{2,3},{3,2},{4,5},{5,4},{6,7},{7,6}} | collective-permute-start | bytes 7962632 | tf_op jit(solution)/shard_map/ppermute | solution.py:425
  1100.4 61.4 %collective-permute-start.55 = (bf16[7,1152,128]{2,1,0:T(8,128)(2,1)}, bf16[7,1152,128]{2,1,0:T(8,128)(2,1)}, u32[]{:S(2)}, u32[]{:S(2)}) collective-permute-start(bf16[7,1152,128]{2,1,0:T(8,128)(2,1)} %collective-permute-done.44.refs_2_), channel_id=1, source_target_pairs={{0,1},{1,0},{2,3},{3,2},{4,5},{5,4},{6,7},{7,6}} | collective-permute-start | bytes 6193160 | tf_op jit(solution)/shard_map/ppermute | solution.py:425
  1101.6 66.6 %collective-permute-start.56 = (bf16[7,1152,128]{2,1,0:T(8,128)(2,1)}, bf16[7,1152,128]{2,1,0:T(8,128)(2,1)}, u32[]{:S(2)}, u32[]{:S(2)}) collective-permute-start(bf16[7,1152,128]{2,1,0:T(8,128)(2,1)} %collective-permute-done.45.refs_4_), channel_id=1, source_target_pairs={{0,1},{1,0},{2,3},{3,2},{4,5},{5,4},{6,7},{7,6}} | collective-permute-start | bytes 6193160 | tf_op jit(solution)/shard_map/ppermute | solution.py:425
  1105.6 54.4 %collective-permute-start.25 = (bf16[4,1152,128]{2,1,0:T(8,128)(2,1)}, bf16[4,1152,128]{2,1,0:T(8,128)(2,1)}, u32[]{:S(2)}, u32[]{:S(2)}) collective-permute-start(bf16[4,1152,128]{2,1,0:T(8,128)(2,1)} %get-tuple-element.981), channel_id=1, source_target_pairs={{0,4},{1,5},{2,6},{3,7},{4,0},{5,1},{6,2},{7,3}} | collective-permute-start | bytes 3538952 | tf_op jit(solution)/shard_map/ppermute | solution.py:425
  1108.9 51.1 %collective-permute-start.27 = (bf16[4,1152,128]{2,1,0:T(8,128)(2,1)}, bf16[4,1152,128]{2,1,0:T(8,128)(2,1)}, u32[]{:S(2)}, u32[]{:S(2)}) collective-permute-start(bf16[4,1152,128]{2,1,0:T(8,128)(2,1)} %get-tuple-element.982), channel_id=1, source_target_pairs={{0,6},{1,7},{2,4},{3,5}} | collective-permute-start | bytes 3538952 | tf_op jit(solution)/shard_map/ppermute | solution.py:425
  1132.7 58.6 %collective-permute-start.67 = (bf16[8,1152,128]{2,1,0:T(8,128)(2,1)}, bf16[8,1152,128]{2,1,0:T(8,128)(2,1)}, u32[]{:S(2)}, u32[]{:S(2)}) collective-permute-start(bf16[8,1152,128]{2,1,0:T(8,128)(2,1)} %copy-done.9), channel_id=1, source_target_pairs={{0,1},{1,0},{2,3},{3,2},{4,5},{5,4},{6,7},{7,6}} | collective-permute-start | bytes 7077896 | tf_op jit(solution)/shard_map/ppermute | solution.py:425
  1191.2 207.8 %collective-permute-start.22 = (bf16[4,1152,128]{2,1,0:T(8,128)(2,1)}, bf16[4,1152,128]{2,1,0:T(8,128)(2,1)}, u32[]{:S(2)}, u32[]{:S(2)}) collective-permute-start(bf16[4,1152,128]{2,1,0:T(8,128)(2,1)} %get-tuple-element.979.refs_0_), channel_id=1, source_target_pairs={{0,1},{1,0},{2,3},{3,2},{4,5},{5,4},{6,7},{7,6}} | collective-permute-start | bytes 3538952 | tf_op jit(solution)/shard_map/ppermute | solution.py:425
  1191.2 207.8 %collective-permute-start.24 = (bf16[4,1152,128]{2,1,0:T(8,128)(2,1)}, bf16[4,1152,128]{2,1,0:T(8,128)(2,1)}, u32[]{:S(2)}, u32[]{:S(2)}) collective-permute-start(bf16[4,1152,128]{2,1,0:T(8,128)(2,1)} %collective-permute-done.23.refs_2_), channel_id=1, source_target_pairs={{0,1},{1,0},{2,3},{3,2},{4,5},{5,4},{6,7},{7,6}} | collective-permute-start | bytes 3538952 | tf_op jit(solution)/shard_map/ppermute | solution.py:425
  1191.7 207.3 %collective-permute-start.26 = (bf16[4,1152,128]{2,1,0:T(8,128)(2,1)}, bf16[4,1152,128]{2,1,0:T(8,128)(2,1)}, u32[]{:S(2)}, u32[]{:S(2)}) collective-permute-start(bf16[4,1152,128]{2,1,0:T(8,128)(2,1)} %collective-permute-done.25.refs_4_), channel_id=1, source_target_pairs={{0,1},{1,0},{2,3},{3,2},{4,5},{5,4},{6,7},{7,6}} | collective-permute-start | bytes 3538952 | tf_op jit(solution)/shard_map/ppermute | solution.py:425
  1191.8 207.3 %collective-permute-start.28 = (bf16[4,1152,128]{2,1,0:T(8,128)(2,1)}, bf16[4,1152,128]{2,1,0:T(8,128)(2,1)}, u32[]{:S(2)}, u32[]{:S(2)}) collective-permute-start(bf16[4,1152,128]{2,1,0:T(8,128)(2,1)} %collective-permute-done.27.refs_6_), channel_id=1, source_target_pairs={{0,1},{1,0},{2,3},{3,2},{4,5},{5,4},{6,7},{7,6}} | collective-permute-start | bytes 3538952 | tf_op jit(solution)/shard_map/ppermute | solution.py:425
  1197.2 201.8 %collective-permute-start.53 = (bf16[2,1152,128]{2,1,0:T(8,128)(2,1)}, bf16[2,1152,128]{2,1,0:T(8,128)(2,1)}, u32[]{:S(2)}, u32[]{:S(2)}) collective-permute-start(bf16[2,1152,128]{2,1,0:T(8,128)(2,1)} %collective-permute-done.52.refs_14_), channel_id=1, source_target_pairs={{0,1},{1,0},{2,3},{3,2},{4,5},{5,4},{6,7},{7,6}} | collective-permute-start | bytes 1769480 | tf_op jit(solution)/shard_map/ppermute | solution.py:425
  (80 other events, 3667.5 us)
where the time goes:
time: 1430 us; the launch traced here: 1410 us
  waiting for transfers between devices  782 us (55%)
  Pallas kernels  409 us (29%)
  starting transfers between devices  144 us (10%)
  local copies, waits for them, and re-layouts  45.8 us (3%)
  other arithmetic  26.8 us (2%)
    ppermute x95, waiting for transfers between devices, send(): return lax.ppermute(x, 'x', pairs)  782 us
    pallas_call x13, Pallas kernels, norm_pack(): pl.pallas_call(kernel, grid_spec=grid_spec, out_shape=[jax.ShapeDtypeStru...  202 us
    pallas_call x12, Pallas kernels, attend(): pl.pallas_call(kernel, in_specs=in_specs, out_specs=out_specs, out_shape=...  192 us
    ppermute x95, starting transfers between devices, send(): return lax.ppermute(x, 'x', pairs)  144 us
  transfers between devices with their start and end apart: 95, of which 25 were waited for; matrix products, arithmetic and copies ran while one was open for 4% of the time, Pallas kernels for 28%

commit v1 on v0

--- a/solution.py
+++ b/solution.py
@@ -71,13 +71,17 @@
     return width, "direct", ALL, NO_3, NO_3
 
 
+def light(width, among):
+    return width, "direct", among, ALL, among
+
+
 def end(width):
     return width, "direct", UP, ALL, UP
 
 
 PLAN = Plan(
     [direct(2), direct(4), direct(6), relay(7), no_chip1(5), relay(6), no_chip1(4), no_3(9)]
-    + [direct(8), direct(8), direct(7), end(4), end(2)]
+    + [direct(8), light(8, ALL[:5]), light(7, ALL[:6]), end(4), end(2)]
 )
 ROOM = PLAN.chunks[SPILL][0]
 EXTRA = 4
@@ -451,7 +455,7 @@
         owns.append(sends[0])
         twins.append(send(sends[0], pairs(ALL, 1)))
         far = send(sends[3], pairs(ALL, 4) if kind == "relay" else pairs(diagonal, 6))
-        near = send(sends[1], pairs(UP, 2) + pairs(LOW, 1) if along == UP else pairs(ALL, 2))
+        near = send(sends[1], pairs(UP, 2) + pairs(LOW, 1) if along == UP else pairs(along, 2))
         over = send(sends[2], pairs(across, 4))
         landed.append([near, over, far])
     state = None

time: 1430 us -> 1430 us (level)
  no operation moved by 1% of the time
where the time goes in v1:
time: 1430 us; the launch traced here: 1410 us
  waiting for transfers between devices  776 us (54%)
  Pallas kernels  409 us (29%)
  starting transfers between devices  151 us (11%)
  local copies, waits for them, and re-layouts  45.8 us (3%)
  other arithmetic  26.8 us (2%)
    ppermute x95, waiting for transfers between devices, send(): return lax.ppermute(x, 'x', pairs)  776 us
    pallas_call x13, Pallas kernels, norm_pack(): pl.pallas_call(kernel, grid_spec=grid_spec, out_shape=[jax.ShapeDtypeStru...  202 us
    pallas_call x12, Pallas kernels, attend(): pl.pallas_call(kernel, in_specs=in_specs, out_specs=out_specs, out_shape=...  192 us
    ppermute x95, starting transfers between devices, send(): return lax.ppermute(x, 'x', pairs)  151 us
  transfers between devices with their start and end apart: 95, of which 25 were waited for; matrix products, arithmetic and copies ran while one was open for 4% of the time, Pallas kernels for 28%

profile of v1, /device:TPU:0, one launch (start us, length us, event | category | flops | bytes accessed | tf_op | source)
XLA Modules:
  0.0 1411.3 jit_solution(135848157206379379)
XLA Ops:
  11.3 6.8 norm_pack.20
  18.1 3.3 collective-permute-start.29
  21.5 11.8 norm_pack.21
  33.4 2.0 collective-permute-start.8
  38.4 73.2 %collective-permute-done.30.refs_4_ = bf16[2,1152,128]{2,1,0:T(8,128)(2,1)S(1)} collective-permute-done((bf16[2,1152,128]{2,1,0:T(8,128)(2,1)S(1)}, bf16[2,1152,128]{2,1,0:T(8,128)(2,1)S(1)}, u32[]{:S(2)}, u32[]{:S(2)}) %collective-permute-start.30) | collective-permute-done | bytes 589856 | tf_op jit(solution)/shard_map/ppermute | solution.py:429
  112.1 16.6 %norm_pack.22 = (bf16[6,1152,128]{2,1,0:T(8,128)(2,1)}, bf16[6,1152,128]{2,1,0:T(8,128)(2,1)}, bf16[6,1152,128]{2,1,0:T(8,128)(2,1)}, bf16[6,1152,128]{2,1,0:T(8,128)(2,1)}) custom-call(s32[288]{0:T(512)} %get-tuple-element.1364.req_ref, s32[288]{0:T(512)} %get-tuple-element.1363.unit_ref, s32[288]{0:T(512)} %fusion.48.ok_ref, bf16[96,768,512]{2,1,0:T(8,128)(2,1)} %c_ref.25, ...), custom_call_target="tpu_custom_call" | custom-call | flops 600000000 | bytes 14155776 | tf_op jit(solution)/shard_map/norm_pack/pallas_call | solution.py:153
  128.8 19.2 %norm_pack.23 = (bf16[7,1152,128]{2,1,0:T(8,128)(2,1)}, bf16[7,1152,128]{2,1,0:T(8,128)(2,1)}, bf16[7,1152,128]{2,1,0:T(8,128)(2,1)}, bf16[7,1152,128]{2,1,0:T(8,128)(2,1)}) custom-call(s32[288]{0:T(512)} %get-tuple-element.1364.req_ref, s32[288]{0:T(512)} %get-tuple-element.1363.unit_ref, s32[288]{0:T(512)} %fusion.48.ok_ref, bf16[96,768,512]{2,1,0:T(8,128)(2,1)} %c_ref.25, ...), custom_call_target="tpu_custom_call" | custom-call | flops 700000000 | bytes 16515072 | tf_op jit(solution)/shard_map/norm_pack/pallas_call | solution.py:153
  149.1 3.0 collective-permute-done.101.refs_7_
  153.9 2.7 collective-permute-start.34
  157.5 36.4 %collective-permute-done.32.refs_2_ = bf16[6,1152,128]{2,1,0:T(8,128)(2,1)} collective-permute-done((bf16[6,1152,128]{2,1,0:T(8,128)(2,1)}, bf16[6,1152,128]{2,1,0:T(8,128)(2,1)}, u32[]{:S(2)}, u32[]{:S(2)}) %collective-permute-start.32) | collective-permute-done | bytes 1769504 | tf_op jit(solution)/shard_map/ppermute | solution.py:429
  193.9 39.7 %collective-permute-done.33.refs_4_ = bf16[6,1152,128]{2,1,0:T(8,128)(2,1)} collective-permute-done((bf16[6,1152,128]{2,1,0:T(8,128)(2,1)}, bf16[6,1152,128]{2,1,0:T(8,128)(2,1)}, u32[]{:S(2)}, u32[]{:S(2)}) %collective-permute-start.33) | collective-permute-done | bytes 1769504 | tf_op jit(solution)/shard_map/ppermute | solution.py:429
  233.6 14.1 norm_pack.24
  247.8 28.3 %collective-permute-done.10.refs_2_ = bf16[7,1152,128]{2,1,0:T(8,128)(2,1)} collective-permute-done((bf16[7,1152,128]{2,1,0:T(8,128)(2,1)}, bf16[7,1152,128]{2,1,0:T(8,128)(2,1)}, u32[]{:S(2)}, u32[]{:S(2)}) %collective-permute-start.10) | collective-permute-done | bytes 2064416 | tf_op jit(solution)/shard_map/ppermute | solution.py:429
  278.0 6.2 collective-permute-start.37
  284.2 69.5 %collective-permute-done.12 = bf16[7,1152,128]{2,1,0:T(8,128)(2,1)} collective-permute-done((bf16[7,1152,128]{2,1,0:T(8,128)(2,1)}, bf16[7,1152,128]{2,1,0:T(8,128)(2,1)}, u32[]{:S(2)}, u32[]{:S(2)}) %collective-permute-start.12) | collective-permute-done | bytes 2064416 | tf_op jit(solution)/shard_map/ppermute | solution.py:429
  354.3 30.5 %collective-permute-done.36.refs_4_ = bf16[5,1152,128]{2,1,0:T(8,128)(2,1)} collective-permute-done((bf16[5,1152,128]{2,1,0:T(8,128)(2,1)}, bf16[5,1152,128]{2,1,0:T(8,128)(2,1)}, u32[]{:S(2)}, u32[]{:S(2)}) %collective-permute-start.36) | collective-permute-done | bytes 1474592 | tf_op jit(solution)/shard_map/ppermute | solution.py:429
  384.8 16.6 %norm_pack.25 = (bf16[6,1152,128]{2,1,0:T(8,128)(2,1)}, bf16[6,1152,128]{2,1,0:T(8,128)(2,1)}, bf16[6,1152,128]{2,1,0:T(8,128)(2,1)}, bf16[6,1152,128]{2,1,0:T(8,128)(2,1)}) custom-call(s32[288]{0:T(512)} %get-tuple-element.1364.req_ref, s32[288]{0:T(512)} %get-tuple-element.1363.unit_ref, s32[288]{0:T(512)} %fusion.48.ok_ref, bf16[96,768,512]{2,1,0:T(8,128)(2,1)} %c_ref.25, ...), custom_call_target="tpu_custom_call" | custom-call | flops 600000000 | bytes 14155776 | tf_op jit(solution)/shard_map/norm_pack/pallas_call | solution.py:153
  404.9 11.6 norm_pack.26
  416.6 26.1 %collective-permute-done.13.refs_2_ = bf16[6,1152,128]{2,1,0:T(8,128)(2,1)S(1)} collective-permute-done((bf16[6,1152,128]{2,1,0:T(8,128)(2,1)}, bf16[6,1152,128]{2,1,0:T(8,128)(2,1)S(1)}, u32[]{:S(2)}, u32[]{:S(2)}) %collective-permute-start.13) | collective-permute-done | bytes 1769504 | tf_op jit(solution)/shard_map/ppermute | solution.py:429
  444.2 37.2 %collective-permute-done.15 = bf16[6,1152,128]{2,1,0:T(8,128)(2,1)} collective-permute-done((bf16[6,1152,128]{2,1,0:T(8,128)(2,1)}, bf16[6,1152,128]{2,1,0:T(8,128)(2,1)}, u32[]{:S(2)}, u32[]{:S(2)}) %collective-permute-start.15) | collective-permute-done | bytes 1769504 | tf_op jit(solution)/shard_map/ppermute | solution.py:429
  481.4 2.2 collective-permute-start.39
  483.6 4.2 collective-permute-start.40
  487.9 49.2 %collective-permute-done.39.refs_4_ = bf16[4,1152,128]{2,1,0:T(8,128)(2,1)S(1)} collective-permute-done((bf16[4,1152,128]{2,1,0:T(8,128)(2,1)}, bf16[4,1152,128]{2,1,0:T(8,128)(2,1)S(1)}, u32[]{:S(2)}, u32[]{:S(2)}) %collective-permute-start.39) | collective-permute-done | bytes 1179680 | tf_op jit(solution)/shard_map/ppermute | solution.py:429
  538.1 24.1 %norm_pack.27 = (bf16[9,1152,128]{2,1,0:T(8,128)(2,1)}, bf16[9,1152,128]{2,1,0:T(8,128)(2,1)}, bf16[9,1152,128]{2,1,0:T(8,128)(2,1)}, bf16[9,1152,128]{2,1,0:T(8,128)(2,1)}) custom-call(s32[288]{0:T(512)} %get-tuple-element.1364.req_ref, s32[288]{0:T(512)} %get-tuple-element.1363.unit_ref, s32[288]{0:T(512)} %fusion.48.ok_ref, bf16[96,768,512]{2,1,0:T(8,128)(2,1)} %c_ref.25, ...), custom_call_target="tpu_custom_call" | custom-call | flops 900000000 | bytes 21233664 | tf_op jit(solution)/shard_map/norm_pack/pallas_call | solution.py:153
  563.4 21.6 %norm_pack.28 = (bf16[8,1152,128]{2,1,0:T(8,128)(2,1)}, bf16[8,1152,128]{2,1,0:T(8,128)(2,1)}, bf16[8,1152,128]{2,1,0:T(8,128)(2,1)}, bf16[8,1152,128]{2,1,0:T(8,128)(2,1)}) custom-call(s32[288]{0:T(512)} %get-tuple-element.1364.req_ref, s32[288]{0:T(512)} %get-tuple-element.1363.unit_ref, s32[288]{0:T(512)} %fusion.48.ok_ref, bf16[96,768,512]{2,1,0:T(8,128)(2,1)} %c_ref.25, ...), custom_call_target="tpu_custom_call" | custom-call | flops 800000000 | bytes 18874368 | tf_op jit(solution)/shard_map/norm_pack/pallas_call | solution.py:153
  585.6 10.5 collective-permute-start.43
  598.4 41.1 %collective-permute-done.41.refs_2_ = bf16[8,1152,128]{2,1,0:T(8,128)(2,1)} collective-permute-done((bf16[8,1152,128]{2,1,0:T(8,128)(2,1)}, bf16[8,1152,128]{2,1,0:T(8,128)(2,1)}, u32[]{:S(2)}, u32[]{:S(2)}) %collective-permute-start.41) | collective-permute-done | bytes 2359328 | tf_op jit(solution)/shard_map/ppermute | solution.py:429
  639.4 9.7 collective-permute-start.17
  649.2 43.7 %collective-permute-start.18 = (bf16[9,1152,128]{2,1,0:T(8,128)(2,1)}, bf16[9,1152,128]{2,1,0:T(8,128)(2,1)}, u32[]{:S(2)}, u32[]{:S(2)}) collective-permute-start(bf16[9,1152,128]{2,1,0:T(8,128)(2,1)} %get-tuple-element.975), channel_id=1, source_target_pairs={{0,6},{1,7},{2,4},{4,2},{5,3},{6,0},{7,1}} | collective-permute-start | bytes 7962632 | tf_op jit(solution)/shard_map/ppermute | solution.py:429
  692.9 4.4 collective-permute-done.43.refs_6_
  697.8 48.6 %collective-permute-done.16.refs_2_ = bf16[9,1152,128]{2,1,0:T(8,128)(2,1)} collective-permute-done((bf16[9,1152,128]{2,1,0:T(8,128)(2,1)}, bf16[9,1152,128]{2,1,0:T(8,128)(2,1)}, u32[]{:S(2)}, u32[]{:S(2)}) %collective-permute-start.16) | collective-permute-done | bytes 2654240 | tf_op jit(solution)/shard_map/ppermute | solution.py:429
  746.4 4.3 collective-permute-done.17.refs_4_
  750.7 56.8 %collective-permute-done.18.refs_6_ = bf16[9,1152,128]{2,1,0:T(8,128)(2,1)} collective-permute-done((bf16[9,1152,128]{2,1,0:T(8,128)(2,1)}, bf16[9,1152,128]{2,1,0:T(8,128)(2,1)}, u32[]{:S(2)}, u32[]{:S(2)}) %collective-permute-start.18) | collective-permute-done | bytes 2654240 | tf_op jit(solution)/shard_map/ppermute | solution.py:429
  807.5 21.6 %norm_pack.29 = (bf16[8,1152,128]{2,1,0:T(8,128)(2,1)}, bf16[8,1152,128]{2,1,0:T(8,128)(2,1)}, bf16[8,1152,128]{2,1,0:T(8,128)(2,1)}, bf16[8,1152,128]{2,1,0:T(8,128)(2,1)}) custom-call(s32[288]{0:T(512)} %get-tuple-element.1364.req_ref, s32[288]{0:T(512)} %get-tuple-element.1363.unit_ref, s32[288]{0:T(512)} %fusion.48.ok_ref, bf16[96,768,512]{2,1,0:T(8,128)(2,1)} %c_ref.25, ...), custom_call_target="tpu_custom_call" | custom-call | flops 800000000 | bytes 18874368 | tf_op jit(solution)/shard_map/norm_pack/pallas_call | solution.py:153
  829.1 19.1 %norm_pack.30 = (bf16[7,1152,128]{2,1,0:T(8,128)(2,1)}, bf16[7,1152,128]{2,1,0:T(8,128)(2,1)}, bf16[7,1152,128]{2,1,0:T(8,128)(2,1)}, bf16[7,1152,128]{2,1,0:T(8,128)(2,1)}) custom-call(s32[288]{0:T(512)} %get-tuple-element.1364.req_ref, s32[288]{0:T(512)} %get-tuple-element.1363.unit_ref, s32[288]{0:T(512)} %fusion.48.ok_ref, bf16[96,768,512]{2,1,0:T(8,128)(2,1)} %c_ref.25, ...), custom_call_target="tpu_custom_call" | custom-call | flops 700000000 | bytes 16515072 | tf_op jit(solution)/shard_map/norm_pack/pallas_call | solution.py:153
  850.2 5.7 collective-permute-start.46
  858.5 39.8 %collective-permute-done.44.refs_2_ = bf16[7,1152,128]{2,1,0:T(8,128)(2,1)} collective-permute-done((bf16[7,1152,128]{2,1,0:T(8,128)(2,1)}, bf16[7,1152,128]{2,1,0:T(8,128)(2,1)}, u32[]{:S(2)}, u32[]{:S(2)}) %collective-permute-start.44) | collective-permute-done | bytes 2064416 | tf_op jit(solution)/shard_map/ppermute | solution.py:429
  898.8 40.2 %collective-permute-done.46.refs_6_ = bf16[7,1152,128]{2,1,0:T(8,128)(2,1)S(1)} collective-permute-done((bf16[7,1152,128]{2,1,0:T(8,128)(2,1)}, bf16[7,1152,128]{2,1,0:T(8,128)(2,1)S(1)}, u32[]{:S(2)}, u32[]{:S(2)}) %collective-permute-start.46) | collective-permute-done | bytes 2064416 | tf_op jit(solution)/shard_map/ppermute | solution.py:429
  938.9 6.4 collective-permute-start.19
  946.8 13.4 collective-permute-start.20
  960.1 5.2 collective-permute-start.21
  965.9 31.6 %collective-permute-done.19.refs_2_ = bf16[8,1152,128]{2,1,0:T(8,128)(2,1)} collective-permute-done((bf16[8,1152,128]{2,1,0:T(8,128)(2,1)S(1)}, bf16[8,1152,128]{2,1,0:T(8,128)(2,1)}, u32[]{:S(2)}, u32[]{:S(2)}) %collective-permute-start.19) | collective-permute-done | bytes 2359328 | tf_op jit(solution)/shard_map/ppermute | solution.py:429
  997.5 62.5 %collective-permute-done.20.refs_4_ = bf16[8,1152,128]{2,1,0:T(8,128)(2,1)} collective-permute-done((bf16[8,1152,128]{2,1,0:T(8,128)(2,1)S(1)}, bf16[8,1152,128]{2,1,0:T(8,128)(2,1)}, u32[]{:S(2)}, u32[]{:S(2)}) %collective-permute-start.20) | collective-permute-done | bytes 2359328 | tf_op jit(solution)/shard_map/ppermute | solution.py:429
  1060.0 11.6 norm_pack.31
  1071.7 6.8 norm_pack.32
  1079.2 11.3 collective-permute-done.48.refs_10_
  1090.4 2.1 collective-permute-start.52
  1107.2 3.3 collective-permute-start.25
  1110.5 3.8 collective-permute-start.27
  1121.6 12.7 collective-permute-done.23.refs_2_
  1134.3 27.3 %collective-permute-done.25.refs_4_ = bf16[4,1152,128]{2,1,0:T(8,128)(2,1)} collective-permute-done((bf16[4,1152,128]{2,1,0:T(8,128)(2,1)}, bf16[4,1152,128]{2,1,0:T(8,128)(2,1)}, u32[]{:S(2)}, u32[]{:S(2)}) %collective-permute-start.25) | collective-permute-done | bytes 1179680 | tf_op jit(solution)/shard_map/ppermute | solution.py:429
  1198.9 14.9 %blank.1 = (bf16[12,6144,512]{2,1,0:T(8,128)(2,1)}, bf16[12,64,6144]{2,1,0:T(8,128)(2,1)}) custom-call(s32[12]{0:T(128)} %dynamic_slice.30.len_ref), custom_call_target="tpu_custom_call" | custom-call | flops 400000000 | bytes 85000000 | tf_op jit(solution)/shard_map/blank/pallas_call | solution.py:319
  1218.6 7.8 attend.19
  1226.4 15.5 %attend.20 = (bf16[12,6144,512]{2,1,0:T(8,128)(2,1)}, bf16[12,64,6144]{2,1,0:T(8,128)(2,1)}, f32[12,128,768]{2,1,0:T(8,128)}) custom-call(s32[12]{0:T(128)} %convert_reduce_fusion.14.count_ref, s32[592]{0:T(1024)} %select_reduce_fusion.2.code_ref, bf16[4,1152,128]{2,1,0:T(8,128)(2,1)} %get-tuple-element.938.refs_0_, ...), custom_call_target="tpu_custom_call", output_to_operand_aliasing={{0}: (12, {}), {1}: (13, {})} | custom-call | flops 200000000 | bytes 4718592 | tf_op jit(solution)/shard_map/attend/pallas_call | solution.py:278
  1241.9 21.7 %attend.21 = (bf16[12,6144,512]{2,1,0:T(8,128)(2,1)}, bf16[12,64,6144]{2,1,0:T(8,128)(2,1)}, f32[12,128,768]{2,1,0:T(8,128)}) custom-call(s32[12]{0:T(128)} %convert_reduce_fusion.14.count_ref, s32[592]{0:T(1024)} %select_reduce_fusion.2.code_ref, bf16[6,1152,128]{2,1,0:T(8,128)(2,1)} %get-tuple-element.1068.refs_0_, ...), custom_call_target="tpu_custom_call", output_to_operand_aliasing={{0}: (12, {}), {1}: (13, {})} | custom-call | flops 200000000 | bytes 4718592 | tf_op jit(solution)/shard_map/attend/pallas_call | solution.py:278
  1263.6 24.4 %attend.22 = (bf16[12,6144,512]{2,1,0:T(8,128)(2,1)}, bf16[12,64,6144]{2,1,0:T(8,128)(2,1)}, f32[12,128,768]{2,1,0:T(8,128)}) custom-call(s32[12]{0:T(128)} %convert_reduce_fusion.14.count_ref, s32[592]{0:T(1024)} %select_reduce_fusion.2.code_ref, bf16[7,1152,128]{2,1,0:T(8,128)(2,1)} %get-tuple-element.1064.refs_0_, ...), custom_call_target="tpu_custom_call", output_to_operand_aliasing={{0}: (12, {}), {1}: (13, {})} | custom-call | flops 200000000 | bytes 4718592 | tf_op jit(solution)/shard_map/attend/pallas_call | solution.py:278
  1288.0 16.2 %attend.23 = (bf16[12,6144,512]{2,1,0:T(8,128)(2,1)}, bf16[12,64,6144]{2,1,0:T(8,128)(2,1)}, f32[12,128,768]{2,1,0:T(8,128)}) custom-call(s32[12]{0:T(128)} %convert_reduce_fusion.14.count_ref, s32[592]{0:T(1024)} %select_reduce_fusion.2.code_ref, bf16[5,1152,128]{2,1,0:T(8,128)(2,1)} %get-tuple-element.1056.refs_0_, ...), custom_call_target="tpu_custom_call", output_to_operand_aliasing={{0}: (12, {}), {1}: (13, {})} | custom-call | flops 200000000 | bytes 4718592 | tf_op jit(solution)/shard_map/attend/pallas_call | solution.py:278
  1304.2 18.2 %attend.24 = (bf16[12,6144,512]{2,1,0:T(8,128)(2,1)}, bf16[12,64,6144]{2,1,0:T(8,128)(2,1)}, f32[12,128,768]{2,1,0:T(8,128)}) custom-call(s32[12]{0:T(128)} %convert_reduce_fusion.14.count_ref, s32[592]{0:T(1024)} %select_reduce_fusion.2.code_ref, bf16[6,1152,128]{2,1,0:T(8,128)(2,1)} %get-tuple-element.1052.refs_0_, ...), custom_call_target="tpu_custom_call", output_to_operand_aliasing={{0}: (12, {}), {1}: (13, {})} | custom-call | flops 200000000 | bytes 4718592 | tf_op jit(solution)/shard_map/attend/pallas_call | solution.py:278
  1322.4 15.5 %attend.25 = (bf16[12,6144,512]{2,1,0:T(8,128)(2,1)}, bf16[12,64,6144]{2,1,0:T(8,128)(2,1)}, f32[12,128,768]{2,1,0:T(8,128)}) custom-call(s32[12]{0:T(128)} %convert_reduce_fusion.14.count_ref, s32[592]{0:T(1024)} %select_reduce_fusion.2.code_ref, bf16[4,1152,128]{2,1,0:T(8,128)(2,1)} %get-tuple-element.1044.refs_0_, ...), custom_call_target="tpu_custom_call", output_to_operand_aliasing={{0}: (12, {}), {1}: (13, {})} | custom-call | flops 200000000 | bytes 4718592 | tf_op jit(solution)/shard_map/attend/pallas_call | solution.py:278
  1337.9 22.3 %attend.26 = (bf16[12,6144,512]{2,1,0:T(8,128)(2,1)}, bf16[12,64,6144]{2,1,0:T(8,128)(2,1)}, f32[12,128,768]{2,1,0:T(8,128)}) custom-call(s32[12]{0:T(128)} %convert_reduce_fusion.14.count_ref, s32[592]{0:T(1024)} %select_reduce_fusion.2.code_ref, bf16[9,1152,128]{2,1,0:T(8,128)(2,1)} %get-tuple-element.1040.refs_0_, ...), custom_call_target="tpu_custom_call", output_to_operand_aliasing={{0}: (12, {}), {1}: (13, {})} | custom-call | flops 200000000 | bytes 4718592 | tf_op jit(solution)/shard_map/attend/pallas_call | solution.py:278
  1360.2 15.5 %attend.27 = (bf16[12,6144,512]{2,1,0:T(8,128)(2,1)}, bf16[12,64,6144]{2,1,0:T(8,128)(2,1)}, f32[12,128,768]{2,1,0:T(8,128)}) custom-call(s32[12]{0:T(128)} %convert_reduce_fusion.14.count_ref, s32[592]{0:T(1024)} %select_reduce_fusion.2.code_ref, bf16[8,1152,128]{2,1,0:T(8,128)(2,1)} %get-tuple-element.1037.refs_0_, ...), custom_call_target="tpu_custom_call", output_to_operand_aliasing={{0}: (14, {}), {1}: (15, {})} | custom-call | flops 200000000 | bytes 4718592 | tf_op jit(solution)/shard_map/attend/pallas_call | solution.py:278
  1375.8 14.1 %attend.28 = (bf16[12,6144,512]{2,1,0:T(8,128)(2,1)}, bf16[12,64,6144]{2,1,0:T(8,128)(2,1)}, f32[12,128,768]{2,1,0:T(8,128)}) custom-call(s32[12]{0:T(128)} %convert_reduce_fusion.14.count_ref, s32[592]{0:T(1024)} %select_reduce_fusion.2.code_ref, bf16[8,1152,128]{2,1,0:T(8,128)(2,1)} %get-tuple-element.1028.refs_0_, ...), custom_call_target="tpu_custom_call", output_to_operand_aliasing={{0}: (12, {}), {1}: (13, {})} | custom-call | flops 200000000 | bytes 4718592 | tf_op jit(solution)/shard_map/attend/pallas_call | solution.py:278
  1389.9 10.7 attend.29
  1400.8 10.3 attend.30
  (363 shorter events, 101.8 us)
Async XLA Ops:
  33.3 95.5 %collective-permute-start.7 = (bf16[4,1152,128]{2,1,0:T(8,128)(2,1)}, bf16[4,1152,128]{2,1,0:T(8,128)(2,1)}, u32[]{:S(2)}, u32[]{:S(2)}) collective-permute-start(bf16[4,1152,128]{2,1,0:T(8,128)(2,1)} %get-tuple-element.964), channel_id=1, source_target_pairs={{0,2},{1,3},{2,0},{3,1},{4,6},{5,7},{6,4},{7,5}} | collective-permute-start | bytes 3538952 | tf_op jit(solution)/shard_map/ppermute | solution.py:429
  33.4 114.7 %collective-permute-start.8 = (bf16[4,1152,128]{2,1,0:T(8,128)(2,1)}, bf16[4,1152,128]{2,1,0:T(8,128)(2,1)}, u32[]{:S(2)}, u32[]{:S(2)}) collective-permute-start(bf16[4,1152,128]{2,1,0:T(8,128)(2,1)} %get-tuple-element.965), channel_id=1, source_target_pairs={{0,4},{1,5},{2,6},{3,7},{4,0},{5,1},{6,2},{7,3}} | collective-permute-start | bytes 3538952 | tf_op jit(solution)/shard_map/ppermute | solution.py:429
  35.4 112.7 %collective-permute-start.9 = (bf16[4,1152,128]{2,1,0:T(8,128)(2,1)}, bf16[4,1152,128]{2,1,0:T(8,128)(2,1)}, u32[]{:S(2)}, u32[]{:S(2)}) collective-permute-start(bf16[4,1152,128]{2,1,0:T(8,128)(2,1)} %get-tuple-element.966), channel_id=1, source_target_pairs={{0,6},{1,7},{2,4},{3,5},{4,2},{5,3},{6,0},{7,1}} | collective-permute-start | bytes 3538952 | tf_op jit(solution)/shard_map/ppermute | solution.py:429
  36.8 74.8 %collective-permute-start.30 = (bf16[2,1152,128]{2,1,0:T(8,128)(2,1)S(1)}, bf16[2,1152,128]{2,1,0:T(8,128)(2,1)S(1)}, u32[]{:S(2)}, u32[]{:S(2)}) collective-permute-start(bf16[2,1152,128]{2,1,0:T(8,128)(2,1)S(1)} %copy-done.49), channel_id=1, source_target_pairs={{0,4},{1,5},{2,6},{3,7},{4,0},{5,1},{6,2},{7,3}} | collective-permute-start | bytes 1769480 | tf_op jit(solution)/shard_map/ppermute | solution.py:429
  38.3 73.2 %collective-permute-start.31 = (bf16[2,1152,128]{2,1,0:T(8,128)(2,1)S(1)}, bf16[2,1152,128]{2,1,0:T(8,128)(2,1)}, u32[]{:S(2)}, u32[]{:S(2)}) collective-permute-start(bf16[2,1152,128]{2,1,0:T(8,128)(2,1)S(1)} %copy-done.48), channel_id=1, source_target_pairs={{0,6},{1,7},{2,4},{3,5},{4,2},{5,3},{6,0},{7,1}} | collective-permute-start | bytes 1769480 | tf_op jit(solution)/shard_map/ppermute | solution.py:429
  111.6 42.3 %collective-permute-start.94 = (bf16[4,1152,128]{2,1,0:T(8,128)(2,1)}, bf16[4,1152,128]{2,1,0:T(8,128)(2,1)}, u32[]{:S(2)}, u32[]{:S(2)}) collective-permute-start(bf16[4,1152,128]{2,1,0:T(8,128)(2,1)} %get-tuple-element.938.refs_0_), channel_id=1, source_target_pairs={{0,1},{1,0},{2,3},{3,2},{4,5},{5,4},{6,7},{7,6}} | collective-permute-start | bytes 3538952 | tf_op jit(solution)/shard_map/ppermute | solution.py:429
  153.9 79.7 %collective-permute-start.33 = (bf16[6,1152,128]{2,1,0:T(8,128)(2,1)}, bf16[6,1152,128]{2,1,0:T(8,128)(2,1)}, u32[]{:S(2)}, u32[]{:S(2)}) collective-permute-start(bf16[6,1152,128]{2,1,0:T(8,128)(2,1)} %get-tuple-element.1006), channel_id=1, source_target_pairs={{0,4},{1,5},{2,6},{3,7},{4,0},{5,1},{6,2},{7,3}} | collective-permute-start | bytes 5308424 | tf_op jit(solution)/shard_map/ppermute | solution.py:429
  153.9 79.7 %collective-permute-start.34 = (bf16[6,1152,128]{2,1,0:T(8,128)(2,1)}, bf16[6,1152,128]{2,1,0:T(8,128)(2,1)}, u32[]{:S(2)}, u32[]{:S(2)}) collective-permute-start(bf16[6,1152,128]{2,1,0:T(8,128)(2,1)} %get-tuple-element.1007), channel_id=1, source_target_pairs={{0,6},{1,7},{2,4},{3,5},{4,2},{5,3},{6,0},{7,1}} | collective-permute-start | bytes 5308424 | tf_op jit(solution)/shard_map/ppermute | solution.py:429
  156.6 119.5 %collective-permute-start.10 = (bf16[7,1152,128]{2,1,0:T(8,128)(2,1)}, bf16[7,1152,128]{2,1,0:T(8,128)(2,1)}, u32[]{:S(2)}, u32[]{:S(2)}) collective-permute-start(bf16[7,1152,128]{2,1,0:T(8,128)(2,1)} %get-tuple-element.967), channel_id=1, source_target_pairs={{0,2},{1,3},{2,0},{3,1},{4,5},{5,4},{6,7},{7,6}} | collective-permute-start | bytes 6193160 | tf_op jit(solution)/shard_map/ppermute | solution.py:429
  157.4 90.4 %collective-permute-start.90 = (bf16[6,1152,128]{2,1,0:T(8,128)(2,1)S(1)}, bf16[6,1152,128]{2,1,0:T(8,128)(2,1)}, u32[]{:S(2)}, u32[]{:S(2)}) collective-permute-start(bf16[6,1152,128]{2,1,0:T(8,128)(2,1)S(1)} %copy-done.8), channel_id=1, source_target_pairs={{0,1},{1,0},{2,3},{3,2},{4,5},{5,4},{6,7},{7,6}} | collective-permute-start | bytes 5308424 | tf_op jit(solution)/shard_map/ppermute | solution.py:429
  193.9 84.1 %collective-permute-start.11 = (bf16[7,1152,128]{2,1,0:T(8,128)(2,1)}, bf16[7,1152,128]{2,1,0:T(8,128)(2,1)}, u32[]{:S(2)}, u32[]{:S(2)}) collective-permute-start(bf16[7,1152,128]{2,1,0:T(8,128)(2,1)} %get-tuple-element.968), channel_id=1, source_target_pairs={{0,4},{1,5},{2,6},{3,7},{4,0},{5,1},{6,2},{7,3}} | collective-permute-start | bytes 6193160 | tf_op jit(solution)/shard_map/ppermute | solution.py:429
  233.6 120.1 %collective-permute-start.12 = (bf16[7,1152,128]{2,1,0:T(8,128)(2,1)}, bf16[7,1152,128]{2,1,0:T(8,128)(2,1)}, u32[]{:S(2)}, u32[]{:S(2)}) collective-permute-start(bf16[7,1152,128]{2,1,0:T(8,128)(2,1)} %get-tuple-element.969), channel_id=1, source_target_pairs={{0,4},{1,5},{2,6},{3,7},{4,0},{5,1},{6,2},{7,3}} | collective-permute-start | bytes 6193160 | tf_op jit(solution)/shard_map/ppermute | solution.py:429
  233.6 120.1 %collective-permute-start.86 = (bf16[7,1152,128]{2,1,0:T(8,128)(2,1)}, bf16[7,1152,128]{2,1,0:T(8,128)(2,1)}, u32[]{:S(2)}, u32[]{:S(2)}) collective-permute-start(bf16[7,1152,128]{2,1,0:T(8,128)(2,1)} %get-tuple-element.1064.refs_0_), channel_id=1, source_target_pairs={{0,1},{1,0},{2,3},{3,2},{4,5},{5,4},{6,7},{7,6}} | collective-permute-start | bytes 6193160 | tf_op jit(solution)/shard_map/ppermute | solution.py:429
  247.8 106.4 %collective-permute-start.35 = (bf16[5,1152,128]{2,1,0:T(8,128)(2,1)}, bf16[5,1152,128]{2,1,0:T(8,128)(2,1)S(1)}, u32[]{:S(2)}, u32[]{:S(2)}) collective-permute-start(bf16[5,1152,128]{2,1,0:T(8,128)(2,1)} %get-tuple-element.1008), channel_id=1, source_target_pairs={{0,2},{1,3},{2,0},{3,1},{4,6},{5,7},{6,4},{7,5}} | collective-permute-start | bytes 4423688 | tf_op jit(solution)/shard_map/ppermute | solution.py:429
  276.1 108.7 %collective-permute-start.36 = (bf16[5,1152,128]{2,1,0:T(8,128)(2,1)}, bf16[5,1152,128]{2,1,0:T(8,128)(2,1)}, u32[]{:S(2)}, u32[]{:S(2)}) collective-permute-start(bf16[5,1152,128]{2,1,0:T(8,128)(2,1)} %get-tuple-element.1009), channel_id=1, source_target_pairs={{0,4},{1,5},{4,0},{5,1},{6,2},{7,3}} | collective-permute-start | bytes 4423688 | tf_op jit(solution)/shard_map/ppermute | solution.py:429
  278.0 123.4 %collective-permute-start.37 = (bf16[5,1152,128]{2,1,0:T(8,128)(2,1)}, bf16[5,1152,128]{2,1,0:T(8,128)(2,1)}, u32[]{:S(2)}, u32[]{:S(2)}) collective-permute-start(bf16[5,1152,128]{2,1,0:T(8,128)(2,1)} %get-tuple-element.1010), channel_id=1, source_target_pairs={{0,6},{1,7},{4,2},{5,3},{6,0},{7,1}} | collective-permute-start | bytes 4423688 | tf_op jit(solution)/shard_map/ppermute | solution.py:429
  353.7 48.7 %collective-permute-start.91 = (bf16[6,1152,128]{2,1,0:T(8,128)(2,1)}, bf16[6,1152,128]{2,1,0:T(8,128)(2,1)}, u32[]{:S(2)}, u32[]{:S(2)}) collective-permute-start(bf16[6,1152,128]{2,1,0:T(8,128)(2,1)} %collective-permute-done.32.refs_2_), channel_id=1, source_target_pairs={{0,1},{1,0},{2,3},{3,2},{4,5},{5,4},{6,7},{7,6}} | collective-permute-start | bytes 5308424 | tf_op jit(solution)/shard_map/ppermute | solution.py:429
  353.7 48.7 %collective-permute-start.81 = (bf16[5,1152,128]{2,1,0:T(8,128)(2,1)}, bf16[5,1152,128]{2,1,0:T(8,128)(2,1)}, u32[]{:S(2)}, u32[]{:S(2)}) collective-permute-start(bf16[5,1152,128]{2,1,0:T(8,128)(2,1)} %get-tuple-element.1056.refs_0_), channel_id=1, source_target_pairs={{0,1},{1,0},{2,3},{3,2},{4,5},{5,4},{6,7},{7,6}} | collective-permute-start | bytes 4423688 | tf_op jit(solution)/shard_map/ppermute | solution.py:429
  354.2 50.2 %collective-permute-start.92 = (bf16[6,1152,128]{2,1,0:T(8,128)(2,1)}, bf16[6,1152,128]{2,1,0:T(8,128)(2,1)}, u32[]{:S(2)}, u32[]{:S(2)}) collective-permute-start(bf16[6,1152,128]{2,1,0:T(8,128)(2,1)} %collective-permute-done.33.refs_4_), channel_id=1, source_target_pairs={{0,1},{1,0},{2,3},{3,2},{4,5},{5,4},{6,7},{7,6}} | collective-permute-start | bytes 5308424 | tf_op jit(solution)/shard_map/ppermute | solution.py:429
  402.4 79.0 %collective-permute-start.15 = (bf16[6,1152,128]{2,1,0:T(8,128)(2,1)}, bf16[6,1152,128]{2,1,0:T(8,128)(2,1)}, u32[]{:S(2)}, u32[]{:S(2)}) collective-permute-start(bf16[6,1152,128]{2,1,0:T(8,128)(2,1)} %get-tuple-element.972), channel_id=1, source_target_pairs={{0,4},{1,5},{2,6},{3,7},{4,0},{5,1},{6,2},{7,3}} | collective-permute-start | bytes 5308424 | tf_op jit(solution)/shard_map/ppermute | solution.py:429
  404.4 83.4 %collective-permute-start.82 = (bf16[7,1152,128]{2,1,0:T(8,128)(2,1)}, bf16[7,1152,128]{2,1,0:T(8,128)(2,1)}, u32[]{:S(2)}, u32[]{:S(2)}) collective-permute-start(bf16[7,1152,128]{2,1,0:T(8,128)(2,1)} %collective-permute-done.12), channel_id=1, source_target_pairs={{4,6},{5,7},{6,4},{7,5},{0,1},{1,0},{2,3},{3,2}} | collective-permute-start | bytes 6193160 | tf_op jit(solution)/shard_map/ppermute | solution.py:429
  404.4 76.9 %collective-permute-start.77 = (bf16[6,1152,128]{2,1,0:T(8,128)(2,1)}, bf16[6,1152,128]{2,1,0:T(8,128)(2,1)}, u32[]{:S(2)}, u32[]{:S(2)}) collective-permute-start(bf16[6,1152,128]{2,1,0:T(8,128)(2,1)} %get-tuple-element.1052.refs_0_), channel_id=1, source_target_pairs={{0,1},{1,0},{2,3},{3,2},{4,5},{5,4},{6,7},{7,6}} | collective-permute-start | bytes 5308424 | tf_op jit(solution)/shard_map/ppermute | solution.py:429
  444.2 118.7 %collective-permute-start.87 = (bf16[7,1152,128]{2,1,0:T(8,128)(2,1)}, bf16[7,1152,128]{2,1,0:T(8,128)(2,1)}, u32[]{:S(2)}, u32[]{:S(2)}) collective-permute-start(bf16[7,1152,128]{2,1,0:T(8,128)(2,1)} %collective-permute-done.10.refs_2_), channel_id=1, source_target_pairs={{0,1},{1,0},{2,3},{3,2},{4,5},{5,4},{6,7},{7,6}} | collective-permute-start | bytes 6193160 | tf_op jit(solution)/shard_map/ppermute | solution.py:429
  481.4 82.0 %collective-permute-start.88 = (bf16[7,1152,128]{2,1,0:T(8,128)(2,1)}, bf16[7,1152,128]{2,1,0:T(8,128)(2,1)}, u32[]{:S(2)}, u32[]{:S(2)}) collective-permute-start(bf16[7,1152,128]{2,1,0:T(8,128)(2,1)} %collective-permute-done.11.refs_4_), channel_id=1, source_target_pairs={{0,1},{1,0},{2,3},{3,2},{4,5},{5,4},{6,7},{7,6}} | collective-permute-start | bytes 6193160 | tf_op jit(solution)/shard_map/ppermute | solution.py:429
  481.4 55.8 %collective-permute-start.39 = (bf16[4,1152,128]{2,1,0:T(8,128)(2,1)}, bf16[4,1152,128]{2,1,0:T(8,128)(2,1)S(1)}, u32[]{:S(2)}, u32[]{:S(2)}) collective-permute-start(bf16[4,1152,128]{2,1,0:T(8,128)(2,1)} %get-tuple-element.1012), channel_id=1, source_target_pairs={{0,4},{1,5},{4,0},{5,1},{6,2},{7,3}} | collective-permute-start | bytes 3538952 | tf_op jit(solution)/shard_map/ppermute | solution.py:429
  483.6 78.7 %collective-permute-start.40 = (bf16[4,1152,128]{2,1,0:T(8,128)(2,1)}, bf16[4,1152,128]{2,1,0:T(8,128)(2,1)}, u32[]{:S(2)}, u32[]{:S(2)}) collective-permute-start(bf16[4,1152,128]{2,1,0:T(8,128)(2,1)} %get-tuple-element.1013), channel_id=1, source_target_pairs={{0,6},{1,7},{4,2},{5,3},{6,0},{7,1}} | collective-permute-start | bytes 3538952 | tf_op jit(solution)/shard_map/ppermute | solution.py:429
  487.8 75.0 %collective-permute-start.72 = (bf16[4,1152,128]{2,1,0:T(8,128)(2,1)}, bf16[4,1152,128]{2,1,0:T(8,128)(2,1)}, u32[]{:S(2)}, u32[]{:S(2)}) collective-permute-start(bf16[4,1152,128]{2,1,0:T(8,128)(2,1)} %get-tuple-element.1044.refs_0_), channel_id=1, source_target_pairs={{0,1},{1,0},{2,3},{3,2},{4,5},{5,4},{6,7},{7,6}} | collective-permute-start | bytes 3538952 | tf_op jit(solution)/shard_map/ppermute | solution.py:429
  538.1 46.8 %collective-permute-start.83 = (bf16[5,1152,128]{2,1,0:T(8,128)(2,1)S(1)}, bf16[5,1152,128]{2,1,0:T(8,128)(2,1)}, u32[]{:S(2)}, u32[]{:S(2)}) collective-permute-start(bf16[5,1152,128]{2,1,0:T(8,128)(2,1)S(1)} %collective-permute-done.35.refs_2_), channel_id=1, source_target_pairs={{0,1},{1,0},{2,3},{3,2},{4,5},{5,4},{6,7},{7,6}} | collective-permute-start | bytes 4423688 | tf_op jit(solution)/shard_map/ppermute | solution.py:429
  585.0 54.5 %collective-permute-start.41 = (bf16[8,1152,128]{2,1,0:T(8,128)(2,1)}, bf16[8,1152,128]{2,1,0:T(8,128)(2,1)}, u32[]{:S(2)}, u32[]{:S(2)}) collective-permute-start(bf16[8,1152,128]{2,1,0:T(8,128)(2,1)} %get-tuple-element.1014), channel_id=1, source_target_pairs={{0,2},{1,3},{2,0},{3,1},{4,6},{5,7},{6,4},{7,5}} | collective-permute-start | bytes 7077896 | tf_op jit(solution)/shard_map/ppermute | solution.py:429
  585.0 64.1 %collective-permute-start.42 = (bf16[8,1152,128]{2,1,0:T(8,128)(2,1)}, bf16[8,1152,128]{2,1,0:T(8,128)(2,1)}, u32[]{:S(2)}, u32[]{:S(2)}) collective-permute-start(bf16[8,1152,128]{2,1,0:T(8,128)(2,1)} %get-tuple-element.1015), channel_id=1, source_target_pairs={{0,4},{1,5},{2,6},{3,7},{4,0},{5,1},{6,2},{7,3}} | collective-permute-start | bytes 7077896 | tf_op jit(solution)/shard_map/ppermute | solution.py:429
  585.6 111.7 %collective-permute-start.43 = (bf16[8,1152,128]{2,1,0:T(8,128)(2,1)}, bf16[8,1152,128]{2,1,0:T(8,128)(2,1)}, u32[]{:S(2)}, u32[]{:S(2)}) collective-permute-start(bf16[8,1152,128]{2,1,0:T(8,128)(2,1)} %get-tuple-element.1016), channel_id=1, source_target_pairs={{0,6},{1,7},{2,4},{3,5},{4,2},{5,3},{6,0},{7,1}} | collective-permute-start | bytes 7077896 | tf_op jit(solution)/shard_map/ppermute | solution.py:429
  596.1 101.1 %collective-permute-start.63 = (bf16[8,1152,128]{2,1,0:T(8,128)(2,1)}, bf16[8,1152,128]{2,1,0:T(8,128)(2,1)}, u32[]{:S(2)}, u32[]{:S(2)}) collective-permute-start(bf16[8,1152,128]{2,1,0:T(8,128)(2,1)} %get-tuple-element.1037.refs_0_), channel_id=1, source_target_pairs={{0,1},{1,0},{2,3},{3,2},{4,5},{5,4},{6,7},{7,6}} | collective-permute-start | bytes 7077896 | tf_op jit(solution)/shard_map/ppermute | solution.py:429
  596.4 150.1 %collective-permute-start.16 = (bf16[9,1152,128]{2,1,0:T(8,128)(2,1)}, bf16[9,1152,128]{2,1,0:T(8,128)(2,1)}, u32[]{:S(2)}, u32[]{:S(2)}) collective-permute-start(bf16[9,1152,128]{2,1,0:T(8,128)(2,1)} %get-tuple-element.973), channel_id=1, source_target_pairs={{0,2},{1,3},{2,0},{3,1},{4,6},{5,7},{6,4},{7,5}} | collective-permute-start | bytes 7962632 | tf_op jit(solution)/shard_map/ppermute | solution.py:429
  639.4 111.3 %collective-permute-start.17 = (bf16[9,1152,128]{2,1,0:T(8,128)(2,1)}, bf16[9,1152,128]{2,1,0:T(8,128)(2,1)}, u32[]{:S(2)}, u32[]{:S(2)}) collective-permute-start(bf16[9,1152,128]{2,1,0:T(8,128)(2,1)} %get-tuple-element.974), channel_id=1, source_target_pairs={{0,4},{1,5},{2,6},{4,0},{5,1},{6,2},{7,3}} | collective-permute-start | bytes 7962632 | tf_op jit(solution)/shard_map/ppermute | solution.py:429
  649.2 158.3 %collective-permute-start.18 = (bf16[9,1152,128]{2,1,0:T(8,128)(2,1)}, bf16[9,1152,128]{2,1,0:T(8,128)(2,1)}, u32[]{:S(2)}, u32[]{:S(2)}) collective-permute-start(bf16[9,1152,128]{2,1,0:T(8,128)(2,1)} %get-tuple-element.975), channel_id=1, source_target_pairs={{0,6},{1,7},{2,4},{4,2},{5,3},{6,0},{7,1}} | collective-permute-start | bytes 7962632 | tf_op jit(solution)/shard_map/ppermute | solution.py:429
  697.3 150.9 %collective-permute-start.68 = (bf16[9,1152,128]{2,1,0:T(8,128)(2,1)}, bf16[9,1152,128]{2,1,0:T(8,128)(2,1)}, u32[]{:S(2)}, u32[]{:S(2)}) collective-permute-start(bf16[9,1152,128]{2,1,0:T(8,128)(2,1)} %get-tuple-element.1040.refs_0_), channel_id=1, source_target_pairs={{0,1},{1,0},{2,3},{3,2},{4,5},{5,4},{6,7},{7,6}} | collective-permute-start | bytes 7962632 | tf_op jit(solution)/shard_map/ppermute | solution.py:429
  697.3 152.9 %collective-permute-start.74 = (bf16[4,1152,128]{2,1,0:T(8,128)(2,1)}, bf16[4,1152,128]{2,1,0:T(8,128)(2,1)S(1)}, u32[]{:S(2)}, u32[]{:S(2)}) collective-permute-start(bf16[4,1152,128]{2,1,0:T(8,128)(2,1)} %copy-done.19), channel_id=1, source_target_pairs={{0,1},{1,0},{2,3},{3,2},{4,5},{5,4},{6,7},{7,6}} | collective-permute-start | bytes 3538952 | tf_op jit(solution)/shard_map/ppermute | solution.py:429
  746.4 103.8 %collective-permute-start.75 = (bf16[4,1152,128]{2,1,0:T(8,128)(2,1)}, bf16[4,1152,128]{2,1,0:T(8,128)(2,1)}, u32[]{:S(2)}, u32[]{:S(2)}) collective-permute-start(bf16[4,1152,128]{2,1,0:T(8,128)(2,1)} %copy-done.20), channel_id=1, source_target_pairs={{0,1},{1,0},{2,3},{3,2},{4,5},{5,4},{6,7},{7,6}} | collective-permute-start | bytes 3538952 | tf_op jit(solution)/shard_map/ppermute | solution.py:429
  750.7 105.2 %collective-permute-start.76 = (bf16[4,1152,128]{2,1,0:T(8,128)(2,1)}, bf16[4,1152,128]{2,1,0:T(8,128)(2,1)}, u32[]{:S(2)}, u32[]{:S(2)}) collective-permute-start(bf16[4,1152,128]{2,1,0:T(8,128)(2,1)} %collective-permute-done.40.refs_6_), channel_id=1, source_target_pairs={{0,1},{1,0},{2,3},{3,2},{4,5},{5,4},{6,7},{7,6}} | collective-permute-start | bytes 3538952 | tf_op jit(solution)/shard_map/ppermute | solution.py:429
  807.5 50.5 %collective-permute-start.80 = (bf16[6,1152,128]{2,1,0:T(8,128)(2,1)}, bf16[6,1152,128]{2,1,0:T(8,128)(2,1)S(1)}, u32[]{:S(2)}, u32[]{:S(2)}) collective-permute-start(bf16[6,1152,128]{2,1,0:T(8,128)(2,1)} %collective-permute-done.73.refs_6_), channel_id=1, source_target_pairs={{0,1},{1,0},{2,3},{3,2},{4,5},{5,4},{6,7},{7,6}} | collective-permute-start | bytes 5308424 | tf_op jit(solution)/shard_map/ppermute | solution.py:429
  848.2 50.0 %collective-permute-start.44 = (bf16[7,1152,128]{2,1,0:T(8,128)(2,1)}, bf16[7,1152,128]{2,1,0:T(8,128)(2,1)}, u32[]{:S(2)}, u32[]{:S(2)}) collective-permute-start(bf16[7,1152,128]{2,1,0:T(8,128)(2,1)} %get-tuple-element.1017), channel_id=1, source_target_pairs={{0,2},{1,3},{2,0},{3,1},{4,6},{5,7}} | collective-permute-start | bytes 6193160 | tf_op jit(solution)/shard_map/ppermute | solution.py:429
  850.2 48.1 %collective-permute-start.45 = (bf16[7,1152,128]{2,1,0:T(8,128)(2,1)}, bf16[7,1152,128]{2,1,0:T(8,128)(2,1)}, u32[]{:S(2)}, u32[]{:S(2)}) collective-permute-start(bf16[7,1152,128]{2,1,0:T(8,128)(2,1)} %get-tuple-element.1018), channel_id=1, source_target_pairs={{0,4},{1,5},{2,6},{3,7},{4,0},{5,1},{6,2},{7,3}} | collective-permute-start | bytes 6193160 | tf_op jit(solution)/shard_map/ppermute | solution.py:429
  850.2 88.7 %collective-permute-start.46 = (bf16[7,1152,128]{2,1,0:T(8,128)(2,1)}, bf16[7,1152,128]{2,1,0:T(8,128)(2,1)S(1)}, u32[]{:S(2)}, u32[]{:S(2)}) collective-permute-start(bf16[7,1152,128]{2,1,0:T(8,128)(2,1)} %get-tuple-element.1019), channel_id=1, source_target_pairs={{0,6},{1,7},{2,4},{3,5},{4,2},{5,3}} | collective-permute-start | bytes 6193160 | tf_op jit(solution)/shard_map/ppermute | solution.py:429
  856.0 83.0 %collective-permute-start.54 = (bf16[7,1152,128]{2,1,0:T(8,128)(2,1)}, bf16[7,1152,128]{2,1,0:T(8,128)(2,1)S(1)}, u32[]{:S(2)}, u32[]{:S(2)}) collective-permute-start(bf16[7,1152,128]{2,1,0:T(8,128)(2,1)} %get-tuple-element.1024.refs_0_), channel_id=1, source_target_pairs={{0,1},{1,0},{2,3},{3,2},{4,5},{5,4},{6,7},{7,6}} | collective-permute-start | bytes 6193160 | tf_op jit(solution)/shard_map/ppermute | solution.py:429
  858.0 87.3 %collective-permute-start.59 = (bf16[8,1152,128]{2,1,0:T(8,128)(2,1)S(1)}, bf16[8,1152,128]{2,1,0:T(8,128)(2,1)S(1)}, u32[]{:S(2)}, u32[]{:S(2)}) collective-permute-start(bf16[8,1152,128]{2,1,0:T(8,128)(2,1)S(1)} %broadcast_select_fusion.1), channel_id=1, source_target_pairs={{4,6},{5,7},{6,4},{7,5},{0,1},{1,0},{2,3},{3,2}} | collective-permute-start | bytes 7077896 | tf_op jit(solution)/shard_map/ppermute | solution.py:429
  898.2 61.9 %collective-permute-start.64 = (bf16[8,1152,128]{2,1,0:T(8,128)(2,1)}, bf16[8,1152,128]{2,1,0:T(8,128)(2,1)}, u32[]{:S(2)}, u32[]{:S(2)}) collective-permute-start(bf16[8,1152,128]{2,1,0:T(8,128)(2,1)} %collective-permute-done.41.refs_2_), channel_id=1, source_target_pairs={{0,1},{1,0},{2,3},{3,2},{4,5},{5,4},{6,7},{7,6}} | collective-permute-start | bytes 7077896 | tf_op jit(solution)/shard_map/ppermute | solution.py:429
  898.2 67.1 %collective-permute-start.65 = (bf16[8,1152,128]{2,1,0:T(8,128)(2,1)}, bf16[8,1152,128]{2,1,0:T(8,128)(2,1)}, u32[]{:S(2)}, u32[]{:S(2)}) collective-permute-start(bf16[8,1152,128]{2,1,0:T(8,128)(2,1)} %collective-permute-done.42.refs_4_), channel_id=1, source_target_pairs={{0,1},{1,0},{2,3},{3,2},{4,5},{5,4},{6,7},{7,6}} | collective-permute-start | bytes 7077896 | tf_op jit(solution)/shard_map/ppermute | solution.py:429
  938.9 58.6 %collective-permute-start.19 = (bf16[8,1152,128]{2,1,0:T(8,128)(2,1)S(1)}, bf16[8,1152,128]{2,1,0:T(8,128)(2,1)}, u32[]{:S(2)}, u32[]{:S(2)}) collective-permute-start(bf16[8,1152,128]{2,1,0:T(8,128)(2,1)S(1)} %copy-done.47), channel_id=1, source_target_pairs={{0,2},{1,3},{2,0},{3,1},{4,6}} | collective-permute-start | bytes 7077896 | tf_op jit(solution)/shard_map/ppermute | solution.py:429
  946.8 113.2 %collective-permute-start.20 = (bf16[8,1152,128]{2,1,0:T(8,128)(2,1)S(1)}, bf16[8,1152,128]{2,1,0:T(8,128)(2,1)}, u32[]{:S(2)}, u32[]{:S(2)}) collective-permute-start(bf16[8,1152,128]{2,1,0:T(8,128)(2,1)S(1)} %copy-done.46), channel_id=1, source_target_pairs={{0,4},{1,5},{2,6},{3,7},{4,0},{5,1},{6,2},{7,3}} | collective-permute-start | bytes 7077896 | tf_op jit(solution)/shard_map/ppermute | solution.py:429
  960.1 118.3 %collective-permute-start.21 = (bf16[8,1152,128]{2,1,0:T(8,128)(2,1)}, bf16[8,1152,128]{2,1,0:T(8,128)(2,1)}, u32[]{:S(2)}, u32[]{:S(2)}) collective-permute-start(bf16[8,1152,128]{2,1,0:T(8,128)(2,1)} %get-tuple-element.978), channel_id=1, source_target_pairs={{0,6},{1,7},{2,4},{3,5},{4,2}} | collective-permute-start | bytes 7077896 | tf_op jit(solution)/shard_map/ppermute | solution.py:429
  965.3 113.2 %collective-permute-start.58 = (bf16[8,1152,128]{2,1,0:T(8,128)(2,1)}, bf16[8,1152,128]{2,1,0:T(8,128)(2,1)}, u32[]{:S(2)}, u32[]{:S(2)}) collective-permute-start(bf16[8,1152,128]{2,1,0:T(8,128)(2,1)} %get-tuple-element.1028.refs_0_), channel_id=1, source_target_pairs={{0,1},{1,0},{2,3},{3,2},{4,5},{5,4},{6,7},{7,6}} | collective-permute-start | bytes 7077896 | tf_op jit(solution)/shard_map/ppermute | solution.py:429
  965.4 137.2 %collective-permute-start.69 = (bf16[9,1152,128]{2,1,0:T(8,128)(2,1)}, bf16[9,1152,128]{2,1,0:T(8,128)(2,1)}, u32[]{:S(2)}, u32[]{:S(2)}) collective-permute-start(bf16[9,1152,128]{2,1,0:T(8,128)(2,1)} %collective-permute-done.16.refs_2_), channel_id=1, source_target_pairs={{0,1},{1,0},{2,3},{3,2},{4,5},{5,4},{6,7},{7,6}} | collective-permute-start | bytes 7962632 | tf_op jit(solution)/shard_map/ppermute | solution.py:429
  997.5 105.7 %collective-permute-start.70 = (bf16[9,1152,128]{2,1,0:T(8,128)(2,1)}, bf16[9,1152,128]{2,1,0:T(8,128)(2,1)}, u32[]{:S(2)}, u32[]{:S(2)}) collective-permute-start(bf16[9,1152,128]{2,1,0:T(8,128)(2,1)} %collective-permute-done.17.refs_4_), channel_id=1, source_target_pairs={{0,1},{1,0},{2,3},{3,2},{4,5},{5,4},{6,7},{7,6}} | collective-permute-start | bytes 7962632 | tf_op jit(solution)/shard_map/ppermute | solution.py:429
  1060.0 45.2 %collective-permute-start.71 = (bf16[9,1152,128]{2,1,0:T(8,128)(2,1)}, bf16[9,1152,128]{2,1,0:T(8,128)(2,1)}, u32[]{:S(2)}, u32[]{:S(2)}) collective-permute-start(bf16[9,1152,128]{2,1,0:T(8,128)(2,1)} %collective-permute-done.18.refs_6_), channel_id=1, source_target_pairs={{0,1},{1,0},{2,3},{3,2},{4,5},{5,4},{6,7},{7,6}} | collective-permute-start | bytes 7962632 | tf_op jit(solution)/shard_map/ppermute | solution.py:429
  1102.1 61.4 %collective-permute-start.55 = (bf16[7,1152,128]{2,1,0:T(8,128)(2,1)}, bf16[7,1152,128]{2,1,0:T(8,128)(2,1)}, u32[]{:S(2)}, u32[]{:S(2)}) collective-permute-start(bf16[7,1152,128]{2,1,0:T(8,128)(2,1)} %collective-permute-done.44.refs_2_), channel_id=1, source_target_pairs={{0,1},{1,0},{2,3},{3,2},{4,5},{5,4},{6,7},{7,6}} | collective-permute-start | bytes 6193160 | tf_op jit(solution)/shard_map/ppermute | solution.py:429
  1103.2 66.6 %collective-permute-start.56 = (bf16[7,1152,128]{2,1,0:T(8,128)(2,1)}, bf16[7,1152,128]{2,1,0:T(8,128)(2,1)}, u32[]{:S(2)}, u32[]{:S(2)}) collective-permute-start(bf16[7,1152,128]{2,1,0:T(8,128)(2,1)} %collective-permute-done.45.refs_4_), channel_id=1, source_target_pairs={{0,1},{1,0},{2,3},{3,2},{4,5},{5,4},{6,7},{7,6}} | collective-permute-start | bytes 6193160 | tf_op jit(solution)/shard_map/ppermute | solution.py:429
  1107.2 54.4 %collective-permute-start.25 = (bf16[4,1152,128]{2,1,0:T(8,128)(2,1)}, bf16[4,1152,128]{2,1,0:T(8,128)(2,1)}, u32[]{:S(2)}, u32[]{:S(2)}) collective-permute-start(bf16[4,1152,128]{2,1,0:T(8,128)(2,1)} %get-tuple-element.981), channel_id=1, source_target_pairs={{0,4},{1,5},{2,6},{3,7},{4,0},{5,1},{6,2},{7,3}} | collective-permute-start | bytes 3538952 | tf_op jit(solution)/shard_map/ppermute | solution.py:429
  1110.5 51.1 %collective-permute-start.27 = (bf16[4,1152,128]{2,1,0:T(8,128)(2,1)}, bf16[4,1152,128]{2,1,0:T(8,128)(2,1)}, u32[]{:S(2)}, u32[]{:S(2)}) collective-permute-start(bf16[4,1152,128]{2,1,0:T(8,128)(2,1)} %get-tuple-element.982), channel_id=1, source_target_pairs={{0,6},{1,7},{2,4},{3,5}} | collective-permute-start | bytes 3538952 | tf_op jit(solution)/shard_map/ppermute | solution.py:429
  1134.3 58.6 %collective-permute-start.67 = (bf16[8,1152,128]{2,1,0:T(8,128)(2,1)}, bf16[8,1152,128]{2,1,0:T(8,128)(2,1)}, u32[]{:S(2)}, u32[]{:S(2)}) collective-permute-start(bf16[8,1152,128]{2,1,0:T(8,128)(2,1)} %copy-done.9), channel_id=1, source_target_pairs={{0,1},{1,0},{2,3},{3,2},{4,5},{5,4},{6,7},{7,6}} | collective-permute-start | bytes 7077896 | tf_op jit(solution)/shard_map/ppermute | solution.py:429
  1192.8 207.8 %collective-permute-start.22 = (bf16[4,1152,128]{2,1,0:T(8,128)(2,1)}, bf16[4,1152,128]{2,1,0:T(8,128)(2,1)}, u32[]{:S(2)}, u32[]{:S(2)}) collective-permute-start(bf16[4,1152,128]{2,1,0:T(8,128)(2,1)} %get-tuple-element.979.refs_0_), channel_id=1, source_target_pairs={{0,1},{1,0},{2,3},{3,2},{4,5},{5,4},{6,7},{7,6}} | collective-permute-start | bytes 3538952 | tf_op jit(solution)/shard_map/ppermute | solution.py:429
  1192.9 207.8 %collective-permute-start.24 = (bf16[4,1152,128]{2,1,0:T(8,128)(2,1)}, bf16[4,1152,128]{2,1,0:T(8,128)(2,1)}, u32[]{:S(2)}, u32[]{:S(2)}) collective-permute-start(bf16[4,1152,128]{2,1,0:T(8,128)(2,1)} %collective-permute-done.23.refs_2_), channel_id=1, source_target_pairs={{0,1},{1,0},{2,3},{3,2},{4,5},{5,4},{6,7},{7,6}} | collective-permute-start | bytes 3538952 | tf_op jit(solution)/shard_map/ppermute | solution.py:429
  1193.4 207.3 %collective-permute-start.26 = (bf16[4,1152,128]{2,1,0:T(8,128)(2,1)}, bf16[4,1152,128]{2,1,0:T(8,128)(2,1)}, u32[]{:S(2)}, u32[]{:S(2)}) collective-permute-start(bf16[4,1152,128]{2,1,0:T(8,128)(2,1)} %collective-permute-done.25.refs_4_), channel_id=1, source_target_pairs={{0,1},{1,0},{2,3},{3,2},{4,5},{5,4},{6,7},{7,6}} | collective-permute-start | bytes 3538952 | tf_op jit(solution)/shard_map/ppermute | solution.py:429
  1193.4 207.3 %collective-permute-start.28 = (bf16[4,1152,128]{2,1,0:T(8,128)(2,1)}, bf16[4,1152,128]{2,1,0:T(8,128)(2,1)}, u32[]{:S(2)}, u32[]{:S(2)}) collective-permute-start(bf16[4,1152,128]{2,1,0:T(8,128)(2,1)} %collective-permute-done.27.refs_6_), channel_id=1, source_target_pairs={{0,1},{1,0},{2,3},{3,2},{4,5},{5,4},{6,7},{7,6}} | collective-permute-start | bytes 3538952 | tf_op jit(solution)/shard_map/ppermute | solution.py:429
  1198.9 201.8 %collective-permute-start.53 = (bf16[2,1152,128]{2,1,0:T(8,128)(2,1)}, bf16[2,1152,128]{2,1,0:T(8,128)(2,1)}, u32[]{:S(2)}, u32[]{:S(2)}) collective-permute-start(bf16[2,1152,128]{2,1,0:T(8,128)(2,1)} %collective-permute-done.52.refs_14_), channel_id=1, source_target_pairs={{0,1},{1,0},{2,3},{3,2},{4,5},{5,4},{6,7},{7,6}} | collective-permute-start | bytes 1769480 | tf_op jit(solution)/shard_map/ppermute | solution.py:429
  (80 other events, 3685.0 us)
